TPU v7x, 32 devices: a whole 2x2x4 slice. The times are simulated.
32 devices in a mesh: dp: 8 (over z, y), mp: 4 (over x, core).
Axes of the slice: x: 2, y: 2, z: 4, core: 2. Of those that a mesh axis runs over, the one named last changes fastest.
Arguments:
- grads: bfloat16 [8, 8, 128, 128], P('dp', None, 'mp'), may hold values from -24 to 24
- weights: bfloat16 [8, 128, 128], P(None, 'mp'), may hold values from -0.5 to 0.5
- moment1: float32 [16, 128, 128], P('dp', 'mp'), may hold values from -6 to 6
- moment2: float32 [16, 128, 128], P('dp', 'mp'), may hold values from 0.25 to 4
- slot_of_block: int32 [8], replicated, may hold values from 0 to 15, as said below
- trainable: int32 [8], replicated, may hold values 0 or 1
- width_of_block: int32 [8], replicated, may hold values from 64 to 128
Outputs:
- moment1_new: float32 [16, 128, 128], P('dp', 'mp')
- moment2_new: float32 [16, 128, 128], P('dp', 'mp')
- weights_new: bfloat16 [8, 128, 128], P(None, 'mp')
- grad_rms: float32 [], replicated
Inputs may be any that keep to these rules, and one draw needn't show every extreme that they name: `slot_of_block`: all values differ; slot s belongs to owner s // 2 of dp; every owner holds at most 2 blocks and some owner exactly 2.
All inputs are finite; a program needn't handle non-finite values.
Results may differ from a plain program's by a relative error of at most 0.001.
Values may be sent and summed in bfloat16 or wider, within the bound.
No kernel may reach another device: no remote copies, remote signals or barrier semaphores. Data moves between devices by JAX's collectives and lax.ppermute only.
A program may use at most 64 MiB of HBM per device.

v0:
```python
import functools

import jax
import jax.numpy as jnp
from jax import lax
from jax.experimental import pallas as pl
from jax.experimental.pallas import tpu as pltpu
from jax.sharding import PartitionSpec as P


STEP = 20
GATHER_BYTES = 4 << 20


F32 = jnp.float32
VMEM_BYTES = 8 << 20
STAGES = [[4], [2], [1]]


def tree_sum(terms):
    while len(terms) > 1:
        terms = [terms[i] + terms[i + 1] for i in range(0, len(terms), 2)]
    return terms[0]


def xor_pairs(size, k):
    return [(j, j ^ k) for j in range(size)]


def live_width(trainable_ref, width_ref, b, block_size):
    width = jnp.clip(width_ref[b], 0, block_size)
    return jnp.where(trainable_ref[b] > 0, width, 0)


def shape_of(*dims, dtype=F32):
    return jax.ShapeDtypeStruct(dims, dtype)


def kernel_call(body, out_shape, scalars, *operands, out_smem=()):
    smem = pl.BlockSpec(memory_space=pltpu.SMEM)
    vmem = pl.BlockSpec(memory_space=pltpu.VMEM)
    return pl.pallas_call(
        body,
        out_shape=out_shape,
        in_specs=[smem] * len(scalars) + [vmem] * len(operands),
        out_specs=tuple(smem if i in out_smem else vmem for i in range(len(out_shape))),
        compiler_params=pltpu.CompilerParams(vmem_limit_bytes=VMEM_BYTES),
    )(*scalars, *operands)


def mask_kernel(trainable_ref, width_ref, weight_ref, live_ref, norm_ref, wide_ref):
    blocks, rows, cols = live_ref.shape
    column = lax.broadcasted_iota(jnp.int32, (rows, cols), 1)
    count = jnp.int32(0)
    for b in range(blocks):
        width = live_width(trainable_ref, width_ref, b, cols)
        count = count + width
        live_ref[b] = (column < width).astype(F32)
        wide_ref[b] = weight_ref[b].astype(F32)
    count = count.astype(F32) * float(cols)
    norm_ref[...] = jnp.sqrt(jnp.full(norm_ref.shape, jnp.maximum(count, 1.0), F32))


def total_kernel(terms, live_ref, *refs):
    grad_refs, total_ref, part_ref = refs[:terms], refs[terms], refs[terms + 1]
    blocks, rows, cols = total_ref.shape
    squares = jnp.zeros((rows, cols), F32)
    for b in range(blocks):
        total = tree_sum([ref[b].astype(F32) for ref in grad_refs])
        total_ref[b] = total
        squares = squares + live_ref[b] * (total * total)
    part_ref[...] = jnp.full(part_ref.shape, jnp.sum(squares), F32)


def placing_kernel(
    order,
    owner_ref,
    slot_ref,
    total_ref,
    live_ref,
    moments_ref,
    block_first_ref,
    block_second_ref,
    slot_total_ref,
    slot_live_ref,
):
    blocks = total_ref.shape[0]
    capacity = slot_total_ref.shape[0]
    owner = owner_ref[0]
    for b in range(blocks):
        slot = slot_ref[b]
        near = (slot // capacity) ^ owner
        near = sum(jnp.where(near == k, order[k], 0) for k in range(len(order)))
        held = slot % capacity
        block_first_ref[b] = moments_ref[near, 0, held]
        block_second_ref[b] = moments_ref[near, 1, held]
    for c in range(capacity):
        block, used = jnp.int32(0), jnp.int32(0)
        for b in range(blocks):
            here = slot_ref[b] == owner * capacity + c
            block = jnp.where(here, b, block)
            used = jnp.where(here, 1, used)
        slot_total_ref[c] = total_ref[block]
        slot_live_ref[c] = live_ref[block] * used.astype(F32)


def step_kernel(parts, *refs):
    part_refs = refs[:parts]
    (
        total_ref,
        live_ref,
        norm_ref,
        wide_ref,
        block_first_ref,
        block_second_ref,
        slot_total_ref,
        slot_live_ref,
        first_ref,
        second_ref,
    ) = refs[parts : parts + 10]
    first_out, second_out, weight_out, rms_out = refs[parts + 10 :]
    blocks = total_ref.shape[0]
    capacity = first_ref.shape[0]

    sumsq = tree_sum([ref[...] for ref in part_refs])
    grad_rms = jnp.sqrt(sumsq) / norm_ref[...]
    clip = (1.0 / jnp.maximum(grad_rms, 1.0))[0:1]

    def moments_of(total, first, second):
        clipped = clip * total
        return 0.9 * first + 0.1 * clipped, 0.95 * second + 0.05 * clipped * clipped

    for b in range(blocks):
        first_new, second_new = moments_of(
            total_ref[b], block_first_ref[b], block_second_ref[b]
        )
        direction = (
            first_new
            / (1.0 - 0.9**STEP)
            / (jnp.sqrt(second_new / (1.0 - 0.95**STEP)) + 1e-08)
        )
        weight = wide_ref[b]
        weight_new = weight - 0.001 * (direction + 0.1 * weight)
        weight_out[b] = jnp.where(live_ref[b] > 0, weight_new, weight).astype(
            weight_out.dtype
        )
    for c in range(capacity):
        first, second = first_ref[c], second_ref[c]
        first_new, second_new = moments_of(slot_total_ref[c], first, second)
        first_out[c] = jnp.where(slot_live_ref[c] > 0, first_new, first)
        second_out[c] = jnp.where(slot_live_ref[c] > 0, second_new, second)
    rms_out[0] = jnp.max(grad_rms)


def gathered(
    replicas,
    shares,
    grads,
    weights,
    moment1,
    moment2,
    slot_of_block,
    trainable,
    width_of_block,
):
    own = grads[0]
    blocks, rows, cols = own.shape
    owner = lax.axis_index("dp").astype(jnp.int32).reshape(1)
    full = (blocks, rows, cols)
    tile = (8, cols)

    def send(x, axis, size, k):
        return lax.ppermute(x, axis, xor_pairs(size, k))

    moments = jnp.stack([moment1, moment2]).astype(jnp.float16)[None]
    offsets = [0]
    carried = own
    for stage, ks in enumerate(STAGES):
        terms = [carried] + [send(carried, "dp", replicas, k) for k in ks]
        moments = jnp.concatenate(
            [moments] + [send(moments, "dp", replicas, k) for k in ks]
        )
        offsets = [k ^ o for k in [0] + ks for o in offsets]
        if stage < len(STAGES) - 1:
            carried = tree_sum([t.astype(F32) for t in terms])
    order = [offsets.index(k) for k in range(replicas)]

    live, norm, wide = kernel_call(
        mask_kernel,
        (shape_of(*full), shape_of(*tile), shape_of(*full)),
        (trainable, width_of_block),
        weights,
    )
    total, part = kernel_call(
        functools.partial(total_kernel, len(terms)),
        (shape_of(*full), shape_of(*tile)),
        (),
        live,
        *terms,
    )
    parts = [part] + [send(part, "mp", shares, k) for k in range(1, shares)]
    placed = kernel_call(
        functools.partial(placing_kernel, order),
        (
            shape_of(*full),
            shape_of(*full),
            shape_of(*moment1.shape),
            shape_of(*moment1.shape),
        ),
        (owner, slot_of_block),
        total,
        live,
        moments.astype(F32),
    )
    first_new, second_new, weights_new, grad_rms = kernel_call(
        functools.partial(step_kernel, shares),
        (
            shape_of(*moment1.shape),
            shape_of(*moment2.shape),
            shape_of(*full, dtype=weights.dtype),
            shape_of(1),
        ),
        (),
        *parts,
        total,
        live,
        norm,
        wide,
        *placed,
        moment1,
        moment2,
        out_smem=(3,),
    )
    return first_new, second_new, weights_new, grad_rms.reshape(())


def reduced(grads, weights, moment1, moment2, slot_of_block, trainable, width_of_block):
    blocks, row_share, block_size = weights.shape
    capacity = moment1.shape[0]
    local_grads = grads[0].reshape(blocks, row_share * block_size)
    own_slots = lax.axis_index("dp") * capacity + jnp.arange(capacity, dtype=jnp.int32)
    owned_onehot = slot_of_block[None, :] == own_slots[:, None]
    columns = jnp.arange(block_size, dtype=jnp.int32)
    live = (
        (trainable[:, None] > 0) & (columns[None, :] < width_of_block[:, None])
    ).astype(F32)
    slot_live = jnp.dot(owned_onehot.astype(F32), live, precision=lax.Precision.HIGHEST)
    count = jnp.sum(live) * block_size
    summed = lax.psum(local_grads.astype(F32), "dp")
    summed_blocks = summed.reshape(blocks, row_share, block_size)
    sumsq = lax.psum(jnp.sum(summed_blocks * summed_blocks * live[:, None, :]), "mp")
    slot_grad = jnp.dot(
        owned_onehot.astype(F32), summed, precision=lax.Precision.HIGHEST
    ).reshape(capacity, row_share, block_size)
    grad_rms = jnp.sqrt(sumsq) / jnp.sqrt(jnp.maximum(count, 1.0))
    clip = 1.0 / jnp.maximum(grad_rms, 1.0)
    update_mask = slot_live[:, None, :] > 0
    clipped = clip * slot_grad
    first_new = jnp.where(update_mask, 0.9 * moment1 + 0.1 * clipped, moment1)
    second_new = jnp.where(
        update_mask, 0.95 * moment2 + 0.05 * clipped * clipped, moment2
    )
    direction = (
        first_new
        / (1.0 - 0.9**STEP)
        / (jnp.sqrt(second_new / (1.0 - 0.95**STEP)) + 1e-08)
    )
    slot_weight = jnp.dot(
        owned_onehot.astype(jnp.bfloat16),
        weights.reshape(blocks, row_share * block_size),
        preferred_element_type=F32,
    ).reshape(capacity, row_share, block_size)
    slot_new = jnp.where(
        update_mask, slot_weight - 0.001 * (direction + 0.1 * slot_weight), slot_weight
    )
    slot_new = slot_new.astype(jnp.bfloat16).reshape(capacity, row_share * block_size)
    every_slot = lax.all_gather(slot_new, "dp", axis=0, tiled=True)
    slots = jnp.arange(every_slot.shape[0], dtype=jnp.int32)
    placing = (slot_of_block[:, None] == slots[None, :]).astype(jnp.bfloat16)
    weights_new = jnp.dot(placing, every_slot, preferred_element_type=F32).astype(
        jnp.bfloat16
    )
    return (
        first_new,
        second_new,
        weights_new.reshape(blocks, row_share, block_size),
        grad_rms,
    )


def local(replicas, shares, grads, *rest):
    two_powers = replicas & (replicas - 1) == 0 and shares & (shares - 1) == 0
    if two_powers and replicas > 1 and replicas * grads.nbytes <= GATHER_BYTES:
        return gathered(replicas, shares, grads, *rest)
    return reduced(grads, *rest)


def solution(mesh):
    return jax.shard_map(
        functools.partial(local, mesh.shape["dp"], mesh.shape["mp"]),
        mesh=mesh,
        in_specs=(
            P("dp", None, "mp", None),
            P(None, "mp", None),
            P("dp", "mp", None),
            P("dp", "mp", None),
            P(),
            P(),
            P(),
        ),
        out_specs=(P("dp", "mp", None), P("dp", "mp", None), P(None, "mp", None), P()),
        check_vma=False,
    )
```

profile of v0, /device:TPU:0, one launch (start us, length us, event | category | flops | bytes accessed | tf_op | source)
XLA Modules:
  0.0 24.3 jit_solution(15947483489888257806)
XLA Ops:
  0.6 4.1 %collective-permute-start = (bf16[8,32,128]{2,1,0:T(8,128)(2,1)}, bf16[8,32,128]{2,1,0:T(8,128)(2,1)S(1)}, u32[]{:S(2)}, u32[]{:S(2)}) collective-permute-start(bf16[8,32,128]{2,1,0:T(8,128)(2,1)} %bitcast.10), channel_id=1, source_target_pairs={{0,16},{4,20},{8,24},{12,28},{16,0},{20,4},{24,8},{28,12},{1,17},{... | collective-permute-start | bytes 196616 | tf_op jit(solution)/shard_map/ppermute | solution.py:173
  4.8 0.8 %convert_bitcast_fusion = (f16[1,1,2,32,128]{4,3,2,1,0:T(8,128)(2,1)S(1)}, f16[1,1,2,32,128]{4,3,2,1,0:T(8,128)(2,1)S(1)}) fusion(f32[2,32,128]{2,1,0:T(8,128)} %refs_13_.1, f32[2,32,128]{2,1,0:T(8,128)} %refs_12_.1), kind=kLoop, calls=%fused_computation.5 | loop fusion | flops 16384 | bytes 98304 | tf_op jit(solution)/shard_map/stack | solution.py:175
  5.6 0.1 collective-permute-start.6
  5.7 3.0 %collective-permute-done = bf16[8,32,128]{2,1,0:T(8,128)(2,1)S(1)} collective-permute-done((bf16[8,32,128]{2,1,0:T(8,128)(2,1)}, bf16[8,32,128]{2,1,0:T(8,128)(2,1)S(1)}, u32[]{:S(2)}, u32[]{:S(2)}) %collective-permute-start) | collective-permute-done | bytes 65568 | tf_op jit(solution)/shard_map/ppermute | solution.py:173
  8.7 1.5 %collective-permute-start.1 = (f32[8,32,128]{2,1,0:T(8,128)S(1)}, f32[8,32,128]{2,1,0:T(8,128)S(1)}, u32[]{:S(2)}, u32[]{:S(2)}) collective-permute-start(f32[8,32,128]{2,1,0:T(8,128)S(1)} %convert_add_fusion), channel_id=1, source_target_pairs={{0,8},{4,12},{8,0},{12,4},{16,24},{20,28},{24,16},{28,20},{1,9},{5... | collective-permute-start | bytes 393224 | tf_op jit(solution)/shard_map/ppermute | solution.py:173
  10.2 0.3 %collective-permute-done.6 = f16[1,2,2,32,128]{4,3,2,1,0:T(8,128)(2,1)S(1)} collective-permute-done((f16[1,2,2,32,128]{4,3,2,1,0:T(8,128)(2,1)S(1)}, f16[1,2,2,32,128]{4,3,2,1,0:T(8,128)(2,1)S(1)}, u32[]{:S(2)}, u32[]{:S(2)}) %collective-permute-start.6) | collective-permute-done | bytes 32800 | tf_op jit(solution)/shard_map/ppermute | solution.py:173
  10.5 1.6 %collective-permute-start.7 = (f16[2,2,2,32,128]{4,3,2,1,0:T(8,128)(2,1)S(1)}, f16[2,2,2,32,128]{4,3,2,1,0:T(8,128)(2,1)S(1)}, u32[]{:S(2)}, u32[]{:S(2)}) collective-permute-start(f16[2,2,2,32,128]{4,3,2,1,0:T(8,128)(2,1)S(1)} %pad_maximum_fusion.1), channel_id=1, source_target_pairs={{0,8},{4,12},{8,0},{12,4},{16,24},{20,28},{24,16},{28,20},{1,9},{5... | collective-permute-start | bytes 196616 | tf_op jit(solution)/shard_map/ppermute | solution.py:173
  12.1 2.4 %collective-permute-done.1 = f32[8,32,128]{2,1,0:T(8,128)S(1)} collective-permute-done((f32[8,32,128]{2,1,0:T(8,128)S(1)}, f32[8,32,128]{2,1,0:T(8,128)S(1)}, u32[]{:S(2)}, u32[]{:S(2)}) %collective-permute-start.1) | collective-permute-done | bytes 131104 | tf_op jit(solution)/shard_map/ppermute | solution.py:173
  14.5 1.7 %collective-permute-start.2 = (f32[8,32,128]{2,1,0:T(8,128)S(1)}, f32[8,32,128]{2,1,0:T(8,128)S(1)}, u32[]{:S(2)}, u32[]{:S(2)}) collective-permute-start(f32[8,32,128]{2,1,0:T(8,128)S(1)} %fusion.refs_0_), channel_id=1, source_target_pairs={{0,4},{4,0},{8,12},{12,8},{16,20},{20,16},{24,28},{28,24},{1,5},{5... | collective-permute-start | bytes 393224 | tf_op jit(solution)/shard_map/ppermute | solution.py:173
  16.3 0.7 %collective-permute-start.8 = (f16[4,2,2,32,128]{4,3,2,1,0:T(8,128)(2,1)S(1)}, f16[4,2,2,32,128]{4,3,2,1,0:T(8,128)(2,1)S(1)}, u32[]{:S(2)}, u32[]{:S(2)}) collective-permute-start(f16[4,2,2,32,128]{4,3,2,1,0:T(8,128)(2,1)S(1)} %pad_maximum_fusion), channel_id=1, source_target_pairs={{0,4},{4,0},{8,12},{12,8},{16,20},{20,16},{24,28},{28,24},{1,5},{5... | collective-permute-start | bytes 393224 | tf_op jit(solution)/shard_map/ppermute | solution.py:173
  17.0 0.6 %copy-done.3 = s32[8]{0:T(128)S(1)} copy-done((s32[8]{0:T(128)S(1)}, s32[8]{0:T(128)}, u32[]{:S(2)}) %copy-start.3) | copy-done | bytes 56
  17.6 0.0 copy-done.4
  17.6 0.6 %shard_map.102 = (f32[8,32,128]{2,1,0:T(8,128)S(1)}, f32[8,128]{1,0:T(8,128)S(1)}, f32[8,32,128]{2,1,0:T(8,128)S(1)}) custom-call(s32[8]{0:T(128)S(1)} %copy-done.3, s32[8]{0:T(128)S(1)} %copy-done.4, bf16[8,32,128]{2,1,0:T(8,128)(2,1)S(1)} %copy-done.2), custom_call_target="tpu_custom_call" | custom-call | tf_op jit(solution)/shard_map/pallas_call | solution.py:42
  18.2 1.3 %collective-permute-done.2.refs_1_ = f32[8,32,128]{2,1,0:T(8,128)S(1)} collective-permute-done((f32[8,32,128]{2,1,0:T(8,128)S(1)}, f32[8,32,128]{2,1,0:T(8,128)S(1)}, u32[]{:S(2)}, u32[]{:S(2)}) %collective-permute-start.2) | collective-permute-done | bytes 131104 | tf_op jit(solution)/shard_map/ppermute | solution.py:173
  19.6 0.1 shard_map.103
  19.7 0.1 collective-permute-start.5
  19.8 1.7 %collective-permute-start.4 = (f32[8,128]{1,0:T(8,128)S(1)}, f32[8,128]{1,0:T(8,128)S(1)}, u32[]{:S(2)}, u32[]{:S(2)}) collective-permute-start(f32[8,128]{1,0:T(8,128)S(1)} %get-tuple-element.18.refs_0_), channel_id=1, source_target_pairs={{0,2},{1,3},{2,0},{3,1},{4,6},{5,7},{6,4},{7,5},{8,10},{9,11},{10,... | collective-permute-start | bytes 12296 | tf_op jit(solution)/shard_map/ppermute | solution.py:173
  21.5 0.1 collective-permute-start.3
  21.6 0.1 maximum_convert_fusion.moments_ref
  21.7 0.0 copy-start.5
  21.7 0.6 %copy-done.5 = s32[8]{0:T(128)S(1)} copy-done((s32[8]{0:T(128)S(1)}, s32[8]{0:T(128)}, u32[]{:S(2)}) %copy-start.5) | copy-done | bytes 56
  22.4 0.7 %shard_map.104 = (f32[8,32,128]{2,1,0:T(8,128)S(1)}, f32[8,32,128]{2,1,0:T(8,128)S(1)}, f32[2,32,128]{2,1,0:T(8,128)S(1)}, f32[2,32,128]{2,1,0:T(8,128)S(1)}) custom-call(s32[1]{0:T(128)} %bitcast.1.owner_ref, s32[8]{0:T(128)S(1)} %copy-done.5, f32[8,32,128]{2,1,0:T(8,128)S(1)} %get-tuple-element.19.total_ref.refs_4_, ...), custom_call_target="tpu_custom_call" | custom-call | tf_op jit(solution)/shard_map/pallas_call | solution.py:42
  23.1 0.4 %collective-permute-done.4.refs_2_ = f32[8,128]{1,0:T(8,128)S(1)} collective-permute-done((f32[8,128]{1,0:T(8,128)S(1)}, f32[8,128]{1,0:T(8,128)S(1)}, u32[]{:S(2)}, u32[]{:S(2)}) %collective-permute-start.4) | collective-permute-done | bytes 4128 | tf_op jit(solution)/shard_map/ppermute | solution.py:173
  23.5 0.8 %shard_map.105 = (f32[2,32,128]{2,1,0:T(8,128)}, f32[2,32,128]{2,1,0:T(8,128)}, bf16[8,32,128]{2,1,0:T(8,128)(2,1)}, f32[1]{0:T(128)}) custom-call(f32[8,128]{1,0:T(8,128)S(1)} %get-tuple-element.18.refs_0_, f32[8,128]{1,0:T(8,128)S(1)} %collective-permute-done.3.refs_1_, f32[8,128]{1,0:T(8,128)S(1)} %collective-permute-done.4.refs_2_, ...), custom_call_target="tpu_custom_call" | custom-call | tf_op jit(solution)/shard_map/pallas_call | solution.py:42
  (19 shorter events, 0.2 us)
Async XLA Ops:
  0.6 8.0 %copy-start.6 = (bf16[1,8,32,128]{3,2,1,0:T(8,128)(2,1)S(1)}, bf16[1,8,32,128]{3,2,1,0:T(8,128)(2,1)}, u32[]{:S(2)}) copy-start(bf16[1,8,32,128]{3,2,1,0:T(8,128)(2,1)} %param.7) | copy-start | bytes 196612
  0.6 8.0 %collective-permute-start = (bf16[8,32,128]{2,1,0:T(8,128)(2,1)}, bf16[8,32,128]{2,1,0:T(8,128)(2,1)S(1)}, u32[]{:S(2)}, u32[]{:S(2)}) collective-permute-start(bf16[8,32,128]{2,1,0:T(8,128)(2,1)} %bitcast.10), channel_id=1, source_target_pairs={{0,16},{4,20},{8,24},{12,28},{16,0},{20,4},{24,8},{28,12},{1,17},{... | collective-permute-start | bytes 196616 | tf_op jit(solution)/shard_map/ppermute | solution.py:173
  5.6 4.9 %collective-permute-start.6 = (f16[1,2,2,32,128]{4,3,2,1,0:T(8,128)(2,1)S(1)}, f16[1,2,2,32,128]{4,3,2,1,0:T(8,128)(2,1)S(1)}, u32[]{:S(2)}, u32[]{:S(2)}) collective-permute-start(f16[1,2,2,32,128]{4,3,2,1,0:T(8,128)(2,1)S(1)} %pad_maximum_fusion.2), channel_id=1, source_target_pairs={{0,16},{4,20},{8,24},{12,28},{16,0},{20,4},{24,8},{28,12},{1,17},{... | collective-permute-start | bytes 98312 | tf_op jit(solution)/shard_map/ppermute | solution.py:173
  8.7 5.8 %collective-permute-start.1 = (f32[8,32,128]{2,1,0:T(8,128)S(1)}, f32[8,32,128]{2,1,0:T(8,128)S(1)}, u32[]{:S(2)}, u32[]{:S(2)}) collective-permute-start(f32[8,32,128]{2,1,0:T(8,128)S(1)} %convert_add_fusion), channel_id=1, source_target_pairs={{0,8},{4,12},{8,0},{12,4},{16,24},{20,28},{24,16},{28,20},{1,9},{5... | collective-permute-start | bytes 393224 | tf_op jit(solution)/shard_map/ppermute | solution.py:173
  10.5 5.8 %collective-permute-start.7 = (f16[2,2,2,32,128]{4,3,2,1,0:T(8,128)(2,1)S(1)}, f16[2,2,2,32,128]{4,3,2,1,0:T(8,128)(2,1)S(1)}, u32[]{:S(2)}, u32[]{:S(2)}) collective-permute-start(f16[2,2,2,32,128]{4,3,2,1,0:T(8,128)(2,1)S(1)} %pad_maximum_fusion.1), channel_id=1, source_target_pairs={{0,8},{4,12},{8,0},{12,4},{16,24},{20,28},{24,16},{28,20},{1,9},{5... | collective-permute-start | bytes 196616 | tf_op jit(solution)/shard_map/ppermute | solution.py:173
  14.5 2.5 %copy-start.2 = (bf16[8,32,128]{2,1,0:T(8,128)(2,1)S(1)}, bf16[8,32,128]{2,1,0:T(8,128)(2,1)}, u32[]{:S(2)}) copy-start(bf16[8,32,128]{2,1,0:T(8,128)(2,1)} %weight_ref.1) | copy-start | bytes 196612
  14.5 5.0 %collective-permute-start.2 = (f32[8,32,128]{2,1,0:T(8,128)S(1)}, f32[8,32,128]{2,1,0:T(8,128)S(1)}, u32[]{:S(2)}, u32[]{:S(2)}) collective-permute-start(f32[8,32,128]{2,1,0:T(8,128)S(1)} %fusion.refs_0_), channel_id=1, source_target_pairs={{0,4},{4,0},{8,12},{12,8},{16,20},{20,16},{24,28},{28,24},{1,5},{5... | collective-permute-start | bytes 393224 | tf_op jit(solution)/shard_map/ppermute | solution.py:173
  16.3 5.3 %collective-permute-start.8 = (f16[4,2,2,32,128]{4,3,2,1,0:T(8,128)(2,1)S(1)}, f16[4,2,2,32,128]{4,3,2,1,0:T(8,128)(2,1)S(1)}, u32[]{:S(2)}, u32[]{:S(2)}) collective-permute-start(f16[4,2,2,32,128]{4,3,2,1,0:T(8,128)(2,1)S(1)} %pad_maximum_fusion), channel_id=1, source_target_pairs={{0,4},{4,0},{8,12},{12,8},{16,20},{20,16},{24,28},{28,24},{1,5},{5... | collective-permute-start | bytes 393224 | tf_op jit(solution)/shard_map/ppermute | solution.py:173
  17.0 0.7 %copy-start.3 = (s32[8]{0:T(128)S(1)}, s32[8]{0:T(128)}, u32[]{:S(2)}) copy-start(s32[8]{0:T(128)} %trainable_ref.1) | copy-start | bytes 100
  17.0 0.7 %copy-start.4 = (s32[8]{0:T(128)S(1)}, s32[8]{0:T(128)}, u32[]{:S(2)}) copy-start(s32[8]{0:T(128)} %width_ref.1) | copy-start | bytes 100
  19.7 3.4 %collective-permute-start.5 = (f32[8,128]{1,0:T(8,128)S(1)}, f32[8,128]{1,0:T(8,128)S(1)}, u32[]{:S(2)}, u32[]{:S(2)}) collective-permute-start(f32[8,128]{1,0:T(8,128)S(1)} %get-tuple-element.18.refs_0_), channel_id=1, source_target_pairs={{0,3},{1,2},{2,1},{3,0},{4,7},{5,6},{6,5},{7,4},{8,11},{9,10},{10,... | collective-permute-start | bytes 12296 | tf_op jit(solution)/shard_map/ppermute | solution.py:173
  19.8 3.7 %collective-permute-start.4 = (f32[8,128]{1,0:T(8,128)S(1)}, f32[8,128]{1,0:T(8,128)S(1)}, u32[]{:S(2)}, u32[]{:S(2)}) collective-permute-start(f32[8,128]{1,0:T(8,128)S(1)} %get-tuple-element.18.refs_0_), channel_id=1, source_target_pairs={{0,2},{1,3},{2,0},{3,1},{4,6},{5,7},{6,4},{7,5},{8,10},{9,11},{10,... | collective-permute-start | bytes 12296 | tf_op jit(solution)/shard_map/ppermute | solution.py:173
  21.5 2.0 %collective-permute-start.3 = (f32[8,128]{1,0:T(8,128)S(1)}, f32[8,128]{1,0:T(8,128)S(1)}, u32[]{:S(2)}, u32[]{:S(2)}) collective-permute-start(f32[8,128]{1,0:T(8,128)S(1)} %get-tuple-element.18.refs_0_), channel_id=1, source_target_pairs={{0,1},{1,0},{2,3},{3,2},{4,5},{5,4},{6,7},{7,6},{8,9},{9,8},{10,11... | collective-permute-start | bytes 12296 | tf_op jit(solution)/shard_map/ppermute | solution.py:173
  21.7 0.7 %copy-start.5 = (s32[8]{0:T(128)S(1)}, s32[8]{0:T(128)}, u32[]{:S(2)}) copy-start(s32[8]{0:T(128)} %slot_ref.1) | copy-start | bytes 100
  22.4 1.1 %copy-start = (f32[2,32,128]{2,1,0:T(8,128)S(1)}, f32[2,32,128]{2,1,0:T(8,128)}, u32[]{:S(2)}) copy-start(f32[2,32,128]{2,1,0:T(8,128)} %refs_13_.1) | copy-start | bytes 98308
  22.4 1.1 %copy-start.1 = (f32[2,32,128]{2,1,0:T(8,128)S(1)}, f32[2,32,128]{2,1,0:T(8,128)}, u32[]{:S(2)}) copy-start(f32[2,32,128]{2,1,0:T(8,128)} %refs_12_.1) | copy-start | bytes 98308
where the time goes:
time: 24.8 us; the launch traced here: 24.3 us
  starting transfers between devices  11.7 us (47%)
  waiting for transfers between devices  7.34 us (30%)
  Pallas kernels  2.21 us (9%)
  local copies, waits for them, and re-layouts  1.34 us (5%)
  other arithmetic  0.97 us (4%)
  between operations  0.74 us (3%)
    ppermute x9, starting transfers between devices, send(): return lax.ppermute(x, axis, xor_pairs(size, k))  11.7 us
    ppermute x9, waiting for transfers between devices, send(): return lax.ppermute(x, axis, xor_pairs(size, k))  7.34 us
    pallas_call x4, Pallas kernels, kernel_call(): pl.pallas_call(body, out_shape=out_shape, in_specs=[smem] * len(scalars)...  2.21 us
    unnamed x14, local copies, waits for them, and re-layouts  1.34 us
    another operation x2, other arithmetic, gathered(): moments = jnp.stack([moment1, moment2]).astype(jnp.float16)[None]  0.79 us
  transfers between devices with their start and end apart: 9, of which 5 were waited for; matrix products, arithmetic and copies ran while one was open for 4% of the time, Pallas kernels for 6%

commit v1 on v0

--- a/solution.py
+++ b/solution.py
@@ -14,7 +14,7 @@
 
 F32 = jnp.float32
 VMEM_BYTES = 8 << 20
-STAGES = [[4], [2], [1]]
+STAGES = [[4, 4], [2, 1], [1, 2]]
 
 
 def tree_sum(terms):
@@ -25,6 +25,14 @@
 
 def xor_pairs(size, k):
     return [(j, j ^ k) for j in range(size)]
+
+
+def staged_pairs(replicas, shares, ks):
+    pairs = []
+    for j in range(replicas):
+        for m in range(shares):
+            pairs.append((j * shares + m, (j ^ ks[m % len(ks)]) * shares + m))
+    return pairs
 
 
 def live_width(trainable_ref, width_ref, b, block_size):
@@ -90,7 +98,10 @@
     for b in range(blocks):
         slot = slot_ref[b]
         near = (slot // capacity) ^ owner
-        near = sum(jnp.where(near == k, order[k], 0) for k in range(len(order)))
+        near = sum(
+            jnp.where(near == k, jnp.where(owner_ref[1] == 0, order[0][k], order[1][k]), 0)
+            for k in range(len(order[0]))
+        )
         held = slot % capacity
         block_first_ref[b] = moments_ref[near, 0, held]
         block_second_ref[b] = moments_ref[near, 1, held]
@@ -165,25 +176,26 @@
 ):
     own = grads[0]
     blocks, rows, cols = own.shape
-    owner = lax.axis_index("dp").astype(jnp.int32).reshape(1)
+    owner = jnp.stack([lax.axis_index("dp"), lax.axis_index("mp") % 2]).astype(jnp.int32)
     full = (blocks, rows, cols)
     tile = (8, cols)
 
     def send(x, axis, size, k):
         return lax.ppermute(x, axis, xor_pairs(size, k))
 
+    def exchange(x, ks):
+        return lax.ppermute(x, ("dp", "mp"), staged_pairs(replicas, shares, ks))
+
     moments = jnp.stack([moment1, moment2]).astype(jnp.float16)[None]
-    offsets = [0]
+    offsets = [[0], [0]]
     carried = own
     for stage, ks in enumerate(STAGES):
-        terms = [carried] + [send(carried, "dp", replicas, k) for k in ks]
-        moments = jnp.concatenate(
-            [moments] + [send(moments, "dp", replicas, k) for k in ks]
-        )
-        offsets = [k ^ o for k in [0] + ks for o in offsets]
+        terms = [carried, exchange(carried, ks)]
+        moments = jnp.concatenate([moments, exchange(moments, ks)])
+        offsets = [[k ^ o for k in (0, ks[i]) for o in offsets[i]] for i in range(2)]
         if stage < len(STAGES) - 1:
             carried = tree_sum([t.astype(F32) for t in terms])
-    order = [offsets.index(k) for k in range(replicas)]
+    order = [[of.index(k) for k in range(replicas)] for of in offsets]
 
     live, norm, wide = kernel_call(
         mask_kernel,

time: 24.8 us -> 24 us (0.968)
  the two profiles are of different devices: /device:TPU:0 before, /device:TPU:1 now
where the time goes in v1:
time: 24 us; the launch traced here: 23.7 us
  starting transfers between devices  15.3 us (64%)
  waiting for transfers between devices  3.12 us (13%)
  Pallas kernels  2.22 us (9%)
  local copies, waits for them, and re-layouts  1.34 us (6%)
  other arithmetic  1.05 us (4%)
  between operations  0.72 us (3%)
    ppermute x6, starting transfers between devices, exchange(): return lax.ppermute(x, ('dp', 'mp'), staged_pairs(replicas, shares, ks))  10.4 us
    ppermute x3, starting transfers between devices, send(): return lax.ppermute(x, axis, xor_pairs(size, k))  4.86 us
    ppermute x6, waiting for transfers between devices, exchange(): return lax.ppermute(x, ('dp', 'mp'), staged_pairs(replicas, shares, ks))  2.58 us
    pallas_call x4, Pallas kernels, kernel_call(): pl.pallas_call(body, out_shape=out_shape, in_specs=[smem] * len(scalars)...  2.22 us
    unnamed x14, local copies, waits for them, and re-layouts  1.34 us
    another operation x2, other arithmetic, gathered(): moments = jnp.stack([moment1, moment2]).astype(jnp.float16)[None]  0.79 us
    ppermute x3, waiting for transfers between devices, send(): return lax.ppermute(x, axis, xor_pairs(size, k))  0.55 us
  transfers between devices with their start and end apart: 9, of which 4 were waited for; matrix products, arithmetic and copies ran while one was open for 4% of the time, Pallas kernels for 6%

profile of v1, /device:TPU:1, one launch (start us, length us, event | category | flops | bytes accessed | tf_op | source)
XLA Modules:
  0.0 23.7 jit_solution(14467947426751811456)
XLA Ops:
  0.6 3.2 %collective-permute-start = (bf16[8,32,128]{2,1,0:T(8,128)(2,1)}, bf16[8,32,128]{2,1,0:T(8,128)(2,1)S(1)}, u32[]{:S(2)}, u32[]{:S(2)}) collective-permute-start(bf16[8,32,128]{2,1,0:T(8,128)(2,1)} %bitcast.11), channel_id=1, source_target_pairs={{0,16},{1,17},{2,18},{3,19},{4,20},{5,21},{6,22},{7,23},{8,24},{9,... | collective-permute-start | bytes 196616 | tf_op jit(solution)/shard_map/ppermute | solution.py:187
  3.8 0.8 %convert_bitcast_fusion = (f16[1,1,2,32,128]{4,3,2,1,0:T(8,128)(2,1)S(1)}, f16[1,1,2,32,128]{4,3,2,1,0:T(8,128)(2,1)S(1)}) fusion(f32[2,32,128]{2,1,0:T(8,128)} %refs_13_.1, f32[2,32,128]{2,1,0:T(8,128)} %refs_12_.1), kind=kLoop, calls=%fused_computation.5 | loop fusion | flops 16384 | bytes 98304 | tf_op jit(solution)/shard_map/stack | solution.py:189
  4.6 0.1 collective-permute-start.6
  4.7 1.0 %collective-permute-done = bf16[8,32,128]{2,1,0:T(8,128)(2,1)S(1)} collective-permute-done((bf16[8,32,128]{2,1,0:T(8,128)(2,1)}, bf16[8,32,128]{2,1,0:T(8,128)(2,1)S(1)}, u32[]{:S(2)}, u32[]{:S(2)}) %collective-permute-start) | collective-permute-done | bytes 65568 | tf_op jit(solution)/shard_map/ppermute | solution.py:187
  5.7 1.4 %collective-permute-start.1 = (f32[8,32,128]{2,1,0:T(8,128)S(1)}, f32[8,32,128]{2,1,0:T(8,128)S(1)}, u32[]{:S(2)}, u32[]{:S(2)}) collective-permute-start(f32[8,32,128]{2,1,0:T(8,128)S(1)} %convert_add_fusion), channel_id=1, source_target_pairs={{0,8},{1,5},{2,10},{3,7},{4,12},{5,1},{6,14},{7,3},{8,0},{9,13},{1... | collective-permute-start | bytes 393224 | tf_op jit(solution)/shard_map/ppermute | solution.py:187
  7.1 1.3 %collective-permute-done.6 = f16[1,2,2,32,128]{4,3,2,1,0:T(8,128)(2,1)S(1)} collective-permute-done((f16[1,2,2,32,128]{4,3,2,1,0:T(8,128)(2,1)S(1)}, f16[1,2,2,32,128]{4,3,2,1,0:T(8,128)(2,1)S(1)}, u32[]{:S(2)}, u32[]{:S(2)}) %collective-permute-start.6) | collective-permute-done | bytes 32800 | tf_op jit(solution)/shard_map/ppermute | solution.py:187
  8.4 1.6 %collective-permute-start.7 = (f16[2,2,2,32,128]{4,3,2,1,0:T(8,128)(2,1)S(1)}, f16[2,2,2,32,128]{4,3,2,1,0:T(8,128)(2,1)S(1)}, u32[]{:S(2)}, u32[]{:S(2)}) collective-permute-start(f16[2,2,2,32,128]{4,3,2,1,0:T(8,128)(2,1)S(1)} %pad_maximum_fusion.1), channel_id=1, source_target_pairs={{0,8},{1,5},{2,10},{3,7},{4,12},{5,1},{6,14},{7,3},{8,0},{9,13},{1... | collective-permute-start | bytes 196616 | tf_op jit(solution)/shard_map/ppermute | solution.py:187
  10.0 3.6 %collective-permute-start.2 = (f32[8,32,128]{2,1,0:T(8,128)S(1)}, f32[8,32,128]{2,1,0:T(8,128)S(1)}, u32[]{:S(2)}, u32[]{:S(2)}) collective-permute-start(f32[8,32,128]{2,1,0:T(8,128)S(1)} %fusion.refs_0_), channel_id=1, source_target_pairs={{0,4},{1,9},{2,6},{3,11},{4,0},{5,13},{6,2},{7,15},{8,12},{9,1},{1... | collective-permute-start | bytes 393224 | tf_op jit(solution)/shard_map/ppermute | solution.py:187
  13.6 0.7 %collective-permute-start.8 = (f16[4,2,2,32,128]{4,3,2,1,0:T(8,128)(2,1)S(1)}, f16[4,2,2,32,128]{4,3,2,1,0:T(8,128)(2,1)S(1)}, u32[]{:S(2)}, u32[]{:S(2)}) collective-permute-start(f16[4,2,2,32,128]{4,3,2,1,0:T(8,128)(2,1)S(1)} %pad_maximum_fusion), channel_id=1, source_target_pairs={{0,4},{1,9},{2,6},{3,11},{4,0},{5,13},{6,2},{7,15},{8,12},{9,1},{1... | collective-permute-start | bytes 393224 | tf_op jit(solution)/shard_map/ppermute | solution.py:187
  14.3 0.1 copy-done.2
  14.4 0.5 %copy-done.3 = s32[8]{0:T(128)S(1)} copy-done((s32[8]{0:T(128)S(1)}, s32[8]{0:T(128)}, u32[]{:S(2)}) %copy-start.3) | copy-done | bytes 56
  14.9 0.0 copy-done.4
  15.0 0.6 %shard_map.102 = (f32[8,32,128]{2,1,0:T(8,128)S(1)}, f32[8,128]{1,0:T(8,128)S(1)}, f32[8,32,128]{2,1,0:T(8,128)S(1)}) custom-call(s32[8]{0:T(128)S(1)} %copy-done.3, s32[8]{0:T(128)S(1)} %copy-done.4, bf16[8,32,128]{2,1,0:T(8,128)(2,1)S(1)} %copy-done.2), custom_call_target="tpu_custom_call" | custom-call | tf_op jit(solution)/shard_map/pallas_call | solution.py:50
  15.5 0.1 pad_add_fusion.owner_ref
  15.6 0.3 %collective-permute-done.2.refs_1_ = f32[8,32,128]{2,1,0:T(8,128)S(1)} collective-permute-done((f32[8,32,128]{2,1,0:T(8,128)S(1)}, f32[8,32,128]{2,1,0:T(8,128)S(1)}, u32[]{:S(2)}, u32[]{:S(2)}) %collective-permute-start.2) | collective-permute-done | bytes 131104 | tf_op jit(solution)/shard_map/ppermute | solution.py:187
  15.9 0.1 shard_map.103
  16.1 4.4 %collective-permute-start.5 = (f32[8,128]{1,0:T(8,128)S(1)}, f32[8,128]{1,0:T(8,128)S(1)}, u32[]{:S(2)}, u32[]{:S(2)}) collective-permute-start(f32[8,128]{1,0:T(8,128)S(1)} %get-tuple-element.18.refs_0_), channel_id=1, source_target_pairs={{0,3},{1,2},{2,1},{3,0},{4,7},{5,6},{6,5},{7,4},{8,11},{9,10},{10,... | collective-permute-start | bytes 12296 | tf_op jit(solution)/shard_map/ppermute | solution.py:184
  20.4 0.5 %collective-permute-start.3 = (f32[8,128]{1,0:T(8,128)S(1)}, f32[8,128]{1,0:T(8,128)S(1)}, u32[]{:S(2)}, u32[]{:S(2)}) collective-permute-start(f32[8,128]{1,0:T(8,128)S(1)} %get-tuple-element.18.refs_0_), channel_id=1, source_target_pairs={{0,1},{1,0},{2,3},{3,2},{4,5},{5,4},{6,7},{7,6},{8,9},{9,8},{10,11... | collective-permute-start | bytes 12296 | tf_op jit(solution)/shard_map/ppermute | solution.py:184
  20.9 0.1 maximum_convert_fusion.moments_ref
  21.0 0.0 copy-start.5
  21.0 0.6 %copy-done.5 = s32[8]{0:T(128)S(1)} copy-done((s32[8]{0:T(128)S(1)}, s32[8]{0:T(128)}, u32[]{:S(2)}) %copy-start.5) | copy-done | bytes 56
  21.7 0.7 %shard_map.104 = (f32[8,32,128]{2,1,0:T(8,128)S(1)}, f32[8,32,128]{2,1,0:T(8,128)S(1)}, f32[2,32,128]{2,1,0:T(8,128)S(1)}, f32[2,32,128]{2,1,0:T(8,128)S(1)}) custom-call(s32[2]{0:T(128)S(1)} %pad_add_fusion.owner_ref, s32[8]{0:T(128)S(1)} %copy-done.5, f32[8,32,128]{2,1,0:T(8,128)S(1)} %get-tuple-element.19.total_ref.refs_4_, ...), custom_call_target="tpu_custom_call" | custom-call | tf_op jit(solution)/shard_map/pallas_call | solution.py:50
  22.4 0.5 %collective-permute-done.4.refs_2_ = f32[8,128]{1,0:T(8,128)S(1)} collective-permute-done((f32[8,128]{1,0:T(8,128)S(1)}, f32[8,128]{1,0:T(8,128)S(1)}, u32[]{:S(2)}, u32[]{:S(2)}) %collective-permute-start.4) | collective-permute-done | bytes 4128 | tf_op jit(solution)/shard_map/ppermute | solution.py:184
  22.9 0.8 %shard_map.105 = (f32[2,32,128]{2,1,0:T(8,128)}, f32[2,32,128]{2,1,0:T(8,128)}, bf16[8,32,128]{2,1,0:T(8,128)(2,1)}, f32[1]{0:T(128)}) custom-call(f32[8,128]{1,0:T(8,128)S(1)} %get-tuple-element.18.refs_0_, f32[8,128]{1,0:T(8,128)S(1)} %collective-permute-done.3.refs_1_, f32[8,128]{1,0:T(8,128)S(1)} %collective-permute-done.4.refs_2_, ...), custom_call_target="tpu_custom_call" | custom-call | tf_op jit(solution)/shard_map/pallas_call | solution.py:50
  (20 shorter events, 0.2 us)
Async XLA Ops:
  0.6 5.1 %copy-start.6 = (bf16[1,8,32,128]{3,2,1,0:T(8,128)(2,1)S(1)}, bf16[1,8,32,128]{3,2,1,0:T(8,128)(2,1)}, u32[]{:S(2)}) copy-start(bf16[1,8,32,128]{3,2,1,0:T(8,128)(2,1)} %param.7) | copy-start | bytes 196612
  0.6 5.1 %collective-permute-start = (bf16[8,32,128]{2,1,0:T(8,128)(2,1)}, bf16[8,32,128]{2,1,0:T(8,128)(2,1)S(1)}, u32[]{:S(2)}, u32[]{:S(2)}) collective-permute-start(bf16[8,32,128]{2,1,0:T(8,128)(2,1)} %bitcast.11), channel_id=1, source_target_pairs={{0,16},{1,17},{2,18},{3,19},{4,20},{5,21},{6,22},{7,23},{8,24},{9,... | collective-permute-start | bytes 196616 | tf_op jit(solution)/shard_map/ppermute | solution.py:187
  4.6 3.7 %collective-permute-start.6 = (f16[1,2,2,32,128]{4,3,2,1,0:T(8,128)(2,1)S(1)}, f16[1,2,2,32,128]{4,3,2,1,0:T(8,128)(2,1)S(1)}, u32[]{:S(2)}, u32[]{:S(2)}) collective-permute-start(f16[1,2,2,32,128]{4,3,2,1,0:T(8,128)(2,1)S(1)} %pad_maximum_fusion.2), channel_id=1, source_target_pairs={{0,16},{1,17},{2,18},{3,19},{4,20},{5,21},{6,22},{7,23},{8,24},{9,... | collective-permute-start | bytes 98312 | tf_op jit(solution)/shard_map/ppermute | solution.py:187
  5.7 4.2 %collective-permute-start.1 = (f32[8,32,128]{2,1,0:T(8,128)S(1)}, f32[8,32,128]{2,1,0:T(8,128)S(1)}, u32[]{:S(2)}, u32[]{:S(2)}) collective-permute-start(f32[8,32,128]{2,1,0:T(8,128)S(1)} %convert_add_fusion), channel_id=1, source_target_pairs={{0,8},{1,5},{2,10},{3,7},{4,12},{5,1},{6,14},{7,3},{8,0},{9,13},{1... | collective-permute-start | bytes 393224 | tf_op jit(solution)/shard_map/ppermute | solution.py:187
  8.4 5.2 %collective-permute-start.7 = (f16[2,2,2,32,128]{4,3,2,1,0:T(8,128)(2,1)S(1)}, f16[2,2,2,32,128]{4,3,2,1,0:T(8,128)(2,1)S(1)}, u32[]{:S(2)}, u32[]{:S(2)}) collective-permute-start(f16[2,2,2,32,128]{4,3,2,1,0:T(8,128)(2,1)S(1)} %pad_maximum_fusion.1), channel_id=1, source_target_pairs={{0,8},{1,5},{2,10},{3,7},{4,12},{5,1},{6,14},{7,3},{8,0},{9,13},{1... | collective-permute-start | bytes 196616 | tf_op jit(solution)/shard_map/ppermute | solution.py:187
  10.0 5.9 %collective-permute-start.2 = (f32[8,32,128]{2,1,0:T(8,128)S(1)}, f32[8,32,128]{2,1,0:T(8,128)S(1)}, u32[]{:S(2)}, u32[]{:S(2)}) collective-permute-start(f32[8,32,128]{2,1,0:T(8,128)S(1)} %fusion.refs_0_), channel_id=1, source_target_pairs={{0,4},{1,9},{2,6},{3,11},{4,0},{5,13},{6,2},{7,15},{8,12},{9,1},{1... | collective-permute-start | bytes 393224 | tf_op jit(solution)/shard_map/ppermute | solution.py:187
  13.6 0.8 %copy-start.2 = (bf16[8,32,128]{2,1,0:T(8,128)(2,1)S(1)}, bf16[8,32,128]{2,1,0:T(8,128)(2,1)}, u32[]{:S(2)}) copy-start(bf16[8,32,128]{2,1,0:T(8,128)(2,1)} %weight_ref.1) | copy-start | bytes 196612
  13.6 7.3 %collective-permute-start.8 = (f16[4,2,2,32,128]{4,3,2,1,0:T(8,128)(2,1)S(1)}, f16[4,2,2,32,128]{4,3,2,1,0:T(8,128)(2,1)S(1)}, u32[]{:S(2)}, u32[]{:S(2)}) collective-permute-start(f16[4,2,2,32,128]{4,3,2,1,0:T(8,128)(2,1)S(1)} %pad_maximum_fusion), channel_id=1, source_target_pairs={{0,4},{1,9},{2,6},{3,11},{4,0},{5,13},{6,2},{7,15},{8,12},{9,1},{1... | collective-permute-start | bytes 393224 | tf_op jit(solution)/shard_map/ppermute | solution.py:187
  14.3 0.7 %copy-start.3 = (s32[8]{0:T(128)S(1)}, s32[8]{0:T(128)}, u32[]{:S(2)}) copy-start(s32[8]{0:T(128)} %trainable_ref.1) | copy-start | bytes 100
  14.3 0.7 %copy-start.4 = (s32[8]{0:T(128)S(1)}, s32[8]{0:T(128)}, u32[]{:S(2)}) copy-start(s32[8]{0:T(128)} %width_ref.1) | copy-start | bytes 100
  16.1 6.3 %collective-permute-start.5 = (f32[8,128]{1,0:T(8,128)S(1)}, f32[8,128]{1,0:T(8,128)S(1)}, u32[]{:S(2)}, u32[]{:S(2)}) collective-permute-start(f32[8,128]{1,0:T(8,128)S(1)} %get-tuple-element.18.refs_0_), channel_id=1, source_target_pairs={{0,3},{1,2},{2,1},{3,0},{4,7},{5,6},{6,5},{7,4},{8,11},{9,10},{10,... | collective-permute-start | bytes 12296 | tf_op jit(solution)/shard_map/ppermute | solution.py:184
  20.4 2.5 %collective-permute-start.4 = (f32[8,128]{1,0:T(8,128)S(1)}, f32[8,128]{1,0:T(8,128)S(1)}, u32[]{:S(2)}, u32[]{:S(2)}) collective-permute-start(f32[8,128]{1,0:T(8,128)S(1)} %get-tuple-element.18.refs_0_), channel_id=1, source_target_pairs={{0,2},{1,3},{2,0},{3,1},{4,6},{5,7},{6,4},{7,5},{8,10},{9,11},{10,... | collective-permute-start | bytes 12296 | tf_op jit(solution)/shard_map/ppermute | solution.py:184
  20.4 2.5 %collective-permute-start.3 = (f32[8,128]{1,0:T(8,128)S(1)}, f32[8,128]{1,0:T(8,128)S(1)}, u32[]{:S(2)}, u32[]{:S(2)}) collective-permute-start(f32[8,128]{1,0:T(8,128)S(1)} %get-tuple-element.18.refs_0_), channel_id=1, source_target_pairs={{0,1},{1,0},{2,3},{3,2},{4,5},{5,4},{6,7},{7,6},{8,9},{9,8},{10,11... | collective-permute-start | bytes 12296 | tf_op jit(solution)/shard_map/ppermute | solution.py:184
  21.0 0.7 %copy-start.5 = (s32[8]{0:T(128)S(1)}, s32[8]{0:T(128)}, u32[]{:S(2)}) copy-start(s32[8]{0:T(128)} %slot_ref.1) | copy-start | bytes 100
  21.7 1.2 %copy-start = (f32[2,32,128]{2,1,0:T(8,128)S(1)}, f32[2,32,128]{2,1,0:T(8,128)}, u32[]{:S(2)}) copy-start(f32[2,32,128]{2,1,0:T(8,128)} %refs_13_.1) | copy-start | bytes 98308
  21.7 1.3 %copy-start.1 = (f32[2,32,128]{2,1,0:T(8,128)S(1)}, f32[2,32,128]{2,1,0:T(8,128)}, u32[]{:S(2)}) copy-start(f32[2,32,128]{2,1,0:T(8,128)} %refs_12_.1) | copy-start | bytes 98308

commit v2 on v1

--- a/solution.py
+++ b/solution.py
@@ -9,12 +9,14 @@
 
 
 STEP = 20
+RATE, DECAY = 0.001, 0.1
 GATHER_BYTES = 4 << 20
 
 
 F32 = jnp.float32
 VMEM_BYTES = 8 << 20
-STAGES = [[4, 4], [2, 1], [1, 2]]
+STAGES = [[4, 1], [2, 2], [1, 4]]
+MSTAGES = [[4, 1], [2, 2], [1, 4]]
 
 
 def tree_sum(terms):
@@ -56,7 +58,7 @@
     )(*scalars, *operands)
 
 
-def mask_kernel(trainable_ref, width_ref, weight_ref, live_ref, norm_ref, wide_ref):
+def mask_kernel(owner_ref, slot_ref, trainable_ref, width_ref, weight_ref, live_ref, norm_ref, wide_ref):
     blocks, rows, cols = live_ref.shape
     column = lax.broadcasted_iota(jnp.int32, (rows, cols), 1)
     count = jnp.int32(0)
@@ -64,7 +66,8 @@
         width = live_width(trainable_ref, width_ref, b, cols)
         count = count + width
         live_ref[b] = (column < width).astype(F32)
-        wide_ref[b] = weight_ref[b].astype(F32)
+        weight = weight_ref[b].astype(F32)
+        wide_ref[b] = jnp.where(column < width, weight * (1.0 - RATE * DECAY), weight)
     count = count.astype(F32) * float(cols)
     norm_ref[...] = jnp.sqrt(jnp.full(norm_ref.shape, jnp.maximum(count, 1.0), F32))
 
@@ -103,8 +106,8 @@
             for k in range(len(order[0]))
         )
         held = slot % capacity
-        block_first_ref[b] = moments_ref[near, 0, held]
-        block_second_ref[b] = moments_ref[near, 1, held]
+        block_first_ref[b] = 0.9 * moments_ref[near, 0, held]
+        block_second_ref[b] = 0.95 * moments_ref[near, 1, held]
     for c in range(capacity):
         block, used = jnp.int32(0), jnp.int32(0)
         for b in range(blocks):
@@ -137,29 +140,19 @@
     grad_rms = jnp.sqrt(sumsq) / norm_ref[...]
     clip = (1.0 / jnp.maximum(grad_rms, 1.0))[0:1]
 
-    def moments_of(total, first, second):
-        clipped = clip * total
-        return 0.9 * first + 0.1 * clipped, 0.95 * second + 0.05 * clipped * clipped
-
-    for b in range(blocks):
-        first_new, second_new = moments_of(
-            total_ref[b], block_first_ref[b], block_second_ref[b]
-        )
-        direction = (
-            first_new
-            / (1.0 - 0.9**STEP)
-            / (jnp.sqrt(second_new / (1.0 - 0.95**STEP)) + 1e-08)
-        )
-        weight = wide_ref[b]
-        weight_new = weight - 0.001 * (direction + 0.1 * weight)
-        weight_out[b] = jnp.where(live_ref[b] > 0, weight_new, weight).astype(
-            weight_out.dtype
-        )
     for c in range(capacity):
         first, second = first_ref[c], second_ref[c]
-        first_new, second_new = moments_of(slot_total_ref[c], first, second)
-        first_out[c] = jnp.where(slot_live_ref[c] > 0, first_new, first)
-        second_out[c] = jnp.where(slot_live_ref[c] > 0, second_new, second)
+        live = slot_live_ref[c] > 0
+        clipped = clip * slot_total_ref[c]
+        first_out[c] = jnp.where(live, 0.9 * first + 0.1 * clipped, first)
+        second_out[c] = jnp.where(live, 0.95 * second + 0.05 * clipped * clipped, second)
+    for b in range(blocks):
+        clipped = clip * total_ref[b]
+        first_new = block_first_ref[b] + 0.1 * clipped
+        second_new = block_second_ref[b] + 0.05 * clipped * clipped
+        spread = jnp.sqrt(second_new * (1.0 / (1.0 - 0.95**STEP))) + 1e-08
+        change = first_new * (RATE / (1.0 - 0.9**STEP)) / spread
+        weight_out[b] = (wide_ref[b] - change * live_ref[b]).astype(weight_out.dtype)
     rms_out[0] = jnp.max(grad_rms)
 
 
@@ -191,8 +184,9 @@
     carried = own
     for stage, ks in enumerate(STAGES):
         terms = [carried, exchange(carried, ks)]
-        moments = jnp.concatenate([moments, exchange(moments, ks)])
-        offsets = [[k ^ o for k in (0, ks[i]) for o in offsets[i]] for i in range(2)]
+        mks = MSTAGES[stage]
+        moments = jnp.concatenate([moments, exchange(moments, mks)])
+        offsets = [[k ^ o for k in (0, mks[i]) for o in offsets[i]] for i in range(2)]
         if stage < len(STAGES) - 1:
             carried = tree_sum([t.astype(F32) for t in terms])
     order = [[of.index(k) for k in range(replicas)] for of in offsets]
@@ -200,7 +194,7 @@
     live, norm, wide = kernel_call(
         mask_kernel,
         (shape_of(*full), shape_of(*tile), shape_of(*full)),
-        (trainable, width_of_block),
+        (owner, slot_of_block, trainable, width_of_block),
         weights,
     )
     total, part = kernel_call(

time: 24 us -> 23.1 us (0.963)
  the two profiles are of different devices: /device:TPU:1 before, /device:TPU:0 now
where the time goes in v2:
time: 23.1 us; the launch traced here: 22.9 us
  starting transfers between devices  13.6 us (59%)
  waiting for transfers between devices  4.65 us (20%)
  Pallas kernels  2.21 us (10%)
  other arithmetic  1.04 us (5%)
  between operations  0.74 us (3%)
  local copies, waits for them, and re-layouts  0.63 us (3%)
    ppermute x6, starting transfers between devices, exchange(): return lax.ppermute(x, ('dp', 'mp'), staged_pairs(replicas, shares, ks))  11.7 us
    ppermute x6, waiting for transfers between devices, exchange(): return lax.ppermute(x, ('dp', 'mp'), staged_pairs(replicas, shares, ks))  3.7 us
    pallas_call x4, Pallas kernels, kernel_call(): pl.pallas_call(body, out_shape=out_shape, in_specs=[smem] * len(scalars)...  2.21 us
    ppermute x3, starting transfers between devices, send(): return lax.ppermute(x, axis, xor_pairs(size, k))  1.92 us
    ppermute x3, waiting for transfers between devices, send(): return lax.ppermute(x, axis, xor_pairs(size, k))  0.95 us
    another operation x2, other arithmetic, gathered(): moments = jnp.stack([moment1, moment2]).astype(jnp.float16)[None]  0.79 us
    unnamed x14, local copies, waits for them, and re-layouts  0.63 us
  transfers between devices with their start and end apart: 9, of which 6 were waited for; matrix products, arithmetic and copies ran while one was open for 5% of the time, Pallas kernels for 6%

profile of v2, /device:TPU:0, one launch (start us, length us, event | category | flops | bytes accessed | tf_op | source)
XLA Modules:
  0.0 22.9 jit_solution(11490046706893200982)
XLA Ops:
  0.6 4.1 %collective-permute-start = (bf16[8,32,128]{2,1,0:T(8,128)(2,1)}, bf16[8,32,128]{2,1,0:T(8,128)(2,1)S(1)}, u32[]{:S(2)}, u32[]{:S(2)}) collective-permute-start(bf16[8,32,128]{2,1,0:T(8,128)(2,1)} %bitcast.11), channel_id=1, source_target_pairs={{0,16},{1,5},{2,18},{3,7},{4,20},{5,1},{6,22},{7,3},{8,24},{9,13},... | collective-permute-start | bytes 196616 | tf_op jit(solution)/shard_map/ppermute | solution.py:180
  4.8 0.8 %convert_bitcast_fusion = (f16[1,1,2,32,128]{4,3,2,1,0:T(8,128)(2,1)S(1)}, f16[1,1,2,32,128]{4,3,2,1,0:T(8,128)(2,1)S(1)}) fusion(f32[2,32,128]{2,1,0:T(8,128)} %refs_13_.1, f32[2,32,128]{2,1,0:T(8,128)} %refs_12_.1), kind=kLoop, calls=%fused_computation.5 | loop fusion | flops 16384 | bytes 98304 | tf_op jit(solution)/shard_map/stack | solution.py:182
  5.6 0.1 collective-permute-start.6
  5.7 1.6 %collective-permute-done = bf16[8,32,128]{2,1,0:T(8,128)(2,1)S(1)} collective-permute-done((bf16[8,32,128]{2,1,0:T(8,128)(2,1)}, bf16[8,32,128]{2,1,0:T(8,128)(2,1)S(1)}, u32[]{:S(2)}, u32[]{:S(2)}) %collective-permute-start) | collective-permute-done | bytes 65568 | tf_op jit(solution)/shard_map/ppermute | solution.py:180
  7.2 2.3 %collective-permute-start.1 = (f32[8,32,128]{2,1,0:T(8,128)S(1)}, f32[8,32,128]{2,1,0:T(8,128)S(1)}, u32[]{:S(2)}, u32[]{:S(2)}) collective-permute-start(f32[8,32,128]{2,1,0:T(8,128)S(1)} %convert_add_fusion), channel_id=1, source_target_pairs={{0,8},{1,9},{2,10},{3,11},{4,12},{5,13},{6,14},{7,15},{8,0},{9,1},... | collective-permute-start | bytes 393224 | tf_op jit(solution)/shard_map/ppermute | solution.py:180
  9.5 1.0 %collective-permute-done.6 = f16[1,2,2,32,128]{4,3,2,1,0:T(8,128)(2,1)S(1)} collective-permute-done((f16[1,2,2,32,128]{4,3,2,1,0:T(8,128)(2,1)S(1)}, f16[1,2,2,32,128]{4,3,2,1,0:T(8,128)(2,1)S(1)}, u32[]{:S(2)}, u32[]{:S(2)}) %collective-permute-start.6) | collective-permute-done | bytes 32800 | tf_op jit(solution)/shard_map/ppermute | solution.py:180
  10.6 1.9 %collective-permute-start.7 = (f16[2,2,2,32,128]{4,3,2,1,0:T(8,128)(2,1)S(1)}, f16[2,2,2,32,128]{4,3,2,1,0:T(8,128)(2,1)S(1)}, u32[]{:S(2)}, u32[]{:S(2)}) collective-permute-start(f16[2,2,2,32,128]{4,3,2,1,0:T(8,128)(2,1)S(1)} %pad_maximum_fusion.1), channel_id=1, source_target_pairs={{0,8},{1,9},{2,10},{3,11},{4,12},{5,13},{6,14},{7,15},{8,0},{9,1},... | collective-permute-start | bytes 196616 | tf_op jit(solution)/shard_map/ppermute | solution.py:180
  12.5 1.7 %collective-permute-start.2 = (f32[8,32,128]{2,1,0:T(8,128)S(1)}, f32[8,32,128]{2,1,0:T(8,128)S(1)}, u32[]{:S(2)}, u32[]{:S(2)}) collective-permute-start(f32[8,32,128]{2,1,0:T(8,128)S(1)} %fusion.refs_0_), channel_id=1, source_target_pairs={{0,4},{1,17},{2,6},{3,19},{4,0},{5,21},{6,2},{7,23},{8,12},{9,25},... | collective-permute-start | bytes 393224 | tf_op jit(solution)/shard_map/ppermute | solution.py:180
  14.2 1.0 %collective-permute-done.7 = f16[2,2,2,32,128]{4,3,2,1,0:T(8,128)(2,1)S(1)} collective-permute-done((f16[2,2,2,32,128]{4,3,2,1,0:T(8,128)(2,1)S(1)}, f16[2,2,2,32,128]{4,3,2,1,0:T(8,128)(2,1)S(1)}, u32[]{:S(2)}, u32[]{:S(2)}) %collective-permute-start.7) | collective-permute-done | bytes 65568 | tf_op jit(solution)/shard_map/ppermute | solution.py:180
  15.3 1.6 %collective-permute-start.8 = (f16[4,2,2,32,128]{4,3,2,1,0:T(8,128)(2,1)S(1)}, f16[4,2,2,32,128]{4,3,2,1,0:T(8,128)(2,1)S(1)}, u32[]{:S(2)}, u32[]{:S(2)}) collective-permute-start(f16[4,2,2,32,128]{4,3,2,1,0:T(8,128)(2,1)S(1)} %pad_maximum_fusion), channel_id=1, source_target_pairs={{0,4},{1,17},{2,6},{3,19},{4,0},{5,21},{6,2},{7,23},{8,12},{9,25},... | collective-permute-start | bytes 393224 | tf_op jit(solution)/shard_map/ppermute | solution.py:180
  16.9 0.1 pad_add_fusion.owner_ref
  17.0 0.6 %copy-done.3 = s32[8]{0:T(128)S(1)} copy-done((s32[8]{0:T(128)S(1)}, s32[8]{0:T(128)}, u32[]{:S(2)}) %copy-start.3) | copy-done | bytes 56
  17.5 0.0 copy-done.4
  17.6 0.6 %shard_map.102 = (f32[8,32,128]{2,1,0:T(8,128)S(1)}, f32[8,128]{1,0:T(8,128)S(1)}, f32[8,32,128]{2,1,0:T(8,128)S(1)}) custom-call(s32[2]{0:T(128)S(1)} %pad_add_fusion.owner_ref, s32[8]{0:T(128)S(1)} %copy-done.3, s32[8]{0:T(128)S(1)} %copy-done.4, s32[8]{0:T(128)S(1)} %copy-done.5, bf16[8,32,128]{2,1,0:T(8,128)(2,1)S(1)} %copy-done.2), custom_call_target="tpu_custom_call" | custom-call | tf_op jit(solution)/shard_map/pallas_call | solution.py:52
  18.2 0.1 shard_map.103
  18.3 0.1 collective-permute-start.5
  18.4 1.6 %collective-permute-start.4 = (f32[8,128]{1,0:T(8,128)S(1)}, f32[8,128]{1,0:T(8,128)S(1)}, u32[]{:S(2)}, u32[]{:S(2)}) collective-permute-start(f32[8,128]{1,0:T(8,128)S(1)} %get-tuple-element.18.refs_0_), channel_id=1, source_target_pairs={{0,2},{1,3},{2,0},{3,1},{4,6},{5,7},{6,4},{7,5},{8,10},{9,11},{10,... | collective-permute-start | bytes 12296 | tf_op jit(solution)/shard_map/ppermute | solution.py:177
  20.0 0.3 %collective-permute-start.3 = (f32[8,128]{1,0:T(8,128)S(1)}, f32[8,128]{1,0:T(8,128)S(1)}, u32[]{:S(2)}, u32[]{:S(2)}) collective-permute-start(f32[8,128]{1,0:T(8,128)S(1)} %get-tuple-element.18.refs_0_), channel_id=1, source_target_pairs={{0,1},{1,0},{2,3},{3,2},{4,5},{5,4},{6,7},{7,6},{8,9},{9,8},{10,11... | collective-permute-start | bytes 12296 | tf_op jit(solution)/shard_map/ppermute | solution.py:177
  20.2 0.1 collective-permute-done.8
  20.3 0.1 maximum_convert_fusion.moments_ref
  20.4 0.7 %shard_map.104 = (f32[8,32,128]{2,1,0:T(8,128)S(1)}, f32[8,32,128]{2,1,0:T(8,128)S(1)}, f32[2,32,128]{2,1,0:T(8,128)S(1)}, f32[2,32,128]{2,1,0:T(8,128)S(1)}) custom-call(s32[2]{0:T(128)S(1)} %pad_add_fusion.owner_ref, s32[8]{0:T(128)S(1)} %copy-done.3, f32[8,32,128]{2,1,0:T(8,128)S(1)} %get-tuple-element.19.total_ref.refs_4_, ...), custom_call_target="tpu_custom_call" | custom-call | tf_op jit(solution)/shard_map/pallas_call | solution.py:52
  21.1 0.3 %collective-permute-done.5.refs_3_ = f32[8,128]{1,0:T(8,128)S(1)} collective-permute-done((f32[8,128]{1,0:T(8,128)S(1)}, f32[8,128]{1,0:T(8,128)S(1)}, u32[]{:S(2)}, u32[]{:S(2)}) %collective-permute-start.5) | collective-permute-done | bytes 4128 | tf_op jit(solution)/shard_map/ppermute | solution.py:177
  21.4 0.7 %collective-permute-done.4.refs_2_ = f32[8,128]{1,0:T(8,128)S(1)} collective-permute-done((f32[8,128]{1,0:T(8,128)S(1)}, f32[8,128]{1,0:T(8,128)S(1)}, u32[]{:S(2)}, u32[]{:S(2)}) %collective-permute-start.4) | collective-permute-done | bytes 4128 | tf_op jit(solution)/shard_map/ppermute | solution.py:177
  22.1 0.8 %shard_map.105 = (f32[2,32,128]{2,1,0:T(8,128)}, f32[2,32,128]{2,1,0:T(8,128)}, bf16[8,32,128]{2,1,0:T(8,128)(2,1)}, f32[1]{0:T(128)}) custom-call(f32[8,128]{1,0:T(8,128)S(1)} %get-tuple-element.18.refs_0_, f32[8,128]{1,0:T(8,128)S(1)} %collective-permute-done.3.refs_1_, f32[8,128]{1,0:T(8,128)S(1)} %collective-permute-done.4.refs_2_, ...), custom_call_target="tpu_custom_call" | custom-call | tf_op jit(solution)/shard_map/pallas_call | solution.py:52
  (20 shorter events, 0.2 us)
Async XLA Ops:
  0.6 6.6 %copy-start.6 = (bf16[1,8,32,128]{3,2,1,0:T(8,128)(2,1)S(1)}, bf16[1,8,32,128]{3,2,1,0:T(8,128)(2,1)}, u32[]{:S(2)}) copy-start(bf16[1,8,32,128]{3,2,1,0:T(8,128)(2,1)} %param.7) | copy-start | bytes 196612
  0.6 6.6 %collective-permute-start = (bf16[8,32,128]{2,1,0:T(8,128)(2,1)}, bf16[8,32,128]{2,1,0:T(8,128)(2,1)S(1)}, u32[]{:S(2)}, u32[]{:S(2)}) collective-permute-start(bf16[8,32,128]{2,1,0:T(8,128)(2,1)} %bitcast.11), channel_id=1, source_target_pairs={{0,16},{1,5},{2,18},{3,7},{4,20},{5,1},{6,22},{7,3},{8,24},{9,13},... | collective-permute-start | bytes 196616 | tf_op jit(solution)/shard_map/ppermute | solution.py:180
  5.6 5.0 %collective-permute-start.6 = (f16[1,2,2,32,128]{4,3,2,1,0:T(8,128)(2,1)S(1)}, f16[1,2,2,32,128]{4,3,2,1,0:T(8,128)(2,1)S(1)}, u32[]{:S(2)}, u32[]{:S(2)}) collective-permute-start(f16[1,2,2,32,128]{4,3,2,1,0:T(8,128)(2,1)S(1)} %pad_maximum_fusion.2), channel_id=1, source_target_pairs={{0,16},{1,5},{2,18},{3,7},{4,20},{5,1},{6,22},{7,3},{8,24},{9,13},... | collective-permute-start | bytes 98312 | tf_op jit(solution)/shard_map/ppermute | solution.py:180
  7.2 5.2 %collective-permute-start.1 = (f32[8,32,128]{2,1,0:T(8,128)S(1)}, f32[8,32,128]{2,1,0:T(8,128)S(1)}, u32[]{:S(2)}, u32[]{:S(2)}) collective-permute-start(f32[8,32,128]{2,1,0:T(8,128)S(1)} %convert_add_fusion), channel_id=1, source_target_pairs={{0,8},{1,9},{2,10},{3,11},{4,12},{5,13},{6,14},{7,15},{8,0},{9,1},... | collective-permute-start | bytes 393224 | tf_op jit(solution)/shard_map/ppermute | solution.py:180
  10.6 4.7 %collective-permute-start.7 = (f16[2,2,2,32,128]{4,3,2,1,0:T(8,128)(2,1)S(1)}, f16[2,2,2,32,128]{4,3,2,1,0:T(8,128)(2,1)S(1)}, u32[]{:S(2)}, u32[]{:S(2)}) collective-permute-start(f16[2,2,2,32,128]{4,3,2,1,0:T(8,128)(2,1)S(1)} %pad_maximum_fusion.1), channel_id=1, source_target_pairs={{0,8},{1,9},{2,10},{3,11},{4,12},{5,13},{6,14},{7,15},{8,0},{9,1},... | collective-permute-start | bytes 196616 | tf_op jit(solution)/shard_map/ppermute | solution.py:180
  12.5 5.7 %collective-permute-start.2 = (f32[8,32,128]{2,1,0:T(8,128)S(1)}, f32[8,32,128]{2,1,0:T(8,128)S(1)}, u32[]{:S(2)}, u32[]{:S(2)}) collective-permute-start(f32[8,32,128]{2,1,0:T(8,128)S(1)} %fusion.refs_0_), channel_id=1, source_target_pairs={{0,4},{1,17},{2,6},{3,19},{4,0},{5,21},{6,2},{7,23},{8,12},{9,25},... | collective-permute-start | bytes 393224 | tf_op jit(solution)/shard_map/ppermute | solution.py:180
  15.2 1.7 %copy-start.2 = (bf16[8,32,128]{2,1,0:T(8,128)(2,1)S(1)}, bf16[8,32,128]{2,1,0:T(8,128)(2,1)}, u32[]{:S(2)}) copy-start(bf16[8,32,128]{2,1,0:T(8,128)(2,1)} %weight_ref.1) | copy-start | bytes 196612
  15.3 5.0 %collective-permute-start.8 = (f16[4,2,2,32,128]{4,3,2,1,0:T(8,128)(2,1)S(1)}, f16[4,2,2,32,128]{4,3,2,1,0:T(8,128)(2,1)S(1)}, u32[]{:S(2)}, u32[]{:S(2)}) collective-permute-start(f16[4,2,2,32,128]{4,3,2,1,0:T(8,128)(2,1)S(1)} %pad_maximum_fusion), channel_id=1, source_target_pairs={{0,4},{1,17},{2,6},{3,19},{4,0},{5,21},{6,2},{7,23},{8,12},{9,25},... | collective-permute-start | bytes 393224 | tf_op jit(solution)/shard_map/ppermute | solution.py:180
  16.9 0.7 %copy-start.3 = (s32[8]{0:T(128)S(1)}, s32[8]{0:T(128)}, u32[]{:S(2)}) copy-start(s32[8]{0:T(128)} %slot_ref.3) | copy-start | bytes 100
  16.9 0.7 %copy-start.4 = (s32[8]{0:T(128)S(1)}, s32[8]{0:T(128)}, u32[]{:S(2)}) copy-start(s32[8]{0:T(128)} %trainable_ref.1) | copy-start | bytes 100
  16.9 0.7 %copy-start.5 = (s32[8]{0:T(128)S(1)}, s32[8]{0:T(128)}, u32[]{:S(2)}) copy-start(s32[8]{0:T(128)} %width_ref.1) | copy-start | bytes 100
  18.3 3.1 %collective-permute-start.5 = (f32[8,128]{1,0:T(8,128)S(1)}, f32[8,128]{1,0:T(8,128)S(1)}, u32[]{:S(2)}, u32[]{:S(2)}) collective-permute-start(f32[8,128]{1,0:T(8,128)S(1)} %get-tuple-element.18.refs_0_), channel_id=1, source_target_pairs={{0,3},{1,2},{2,1},{3,0},{4,7},{5,6},{6,5},{7,4},{8,11},{9,10},{10,... | collective-permute-start | bytes 12296 | tf_op jit(solution)/shard_map/ppermute | solution.py:177
  18.4 3.7 %collective-permute-start.4 = (f32[8,128]{1,0:T(8,128)S(1)}, f32[8,128]{1,0:T(8,128)S(1)}, u32[]{:S(2)}, u32[]{:S(2)}) collective-permute-start(f32[8,128]{1,0:T(8,128)S(1)} %get-tuple-element.18.refs_0_), channel_id=1, source_target_pairs={{0,2},{1,3},{2,0},{3,1},{4,6},{5,7},{6,4},{7,5},{8,10},{9,11},{10,... | collective-permute-start | bytes 12296 | tf_op jit(solution)/shard_map/ppermute | solution.py:177
  20.0 2.1 %collective-permute-start.3 = (f32[8,128]{1,0:T(8,128)S(1)}, f32[8,128]{1,0:T(8,128)S(1)}, u32[]{:S(2)}, u32[]{:S(2)}) collective-permute-start(f32[8,128]{1,0:T(8,128)S(1)} %get-tuple-element.18.refs_0_), channel_id=1, source_target_pairs={{0,1},{1,0},{2,3},{3,2},{4,5},{5,4},{6,7},{7,6},{8,9},{9,8},{10,11... | collective-permute-start | bytes 12296 | tf_op jit(solution)/shard_map/ppermute | solution.py:177
  20.4 1.7 %copy-start = (f32[2,32,128]{2,1,0:T(8,128)S(1)}, f32[2,32,128]{2,1,0:T(8,128)}, u32[]{:S(2)}) copy-start(f32[2,32,128]{2,1,0:T(8,128)} %refs_13_.1) | copy-start | bytes 98308
  20.4 1.7 %copy-start.1 = (f32[2,32,128]{2,1,0:T(8,128)S(1)}, f32[2,32,128]{2,1,0:T(8,128)}, u32[]{:S(2)}) copy-start(f32[2,32,128]{2,1,0:T(8,128)} %refs_12_.1) | copy-start | bytes 98308

commit v3 on v2

--- a/solution.py
+++ b/solution.py
@@ -17,6 +17,13 @@
 VMEM_BYTES = 8 << 20
 STAGES = [[4, 1], [2, 2], [1, 4]]
 MSTAGES = [[4, 1], [2, 2], [1, 4]]
+
+
+def near_moments(moment1, moment2):
+    near = lax.reduce_precision(moment1, exponent_bits=5, mantissa_bits=10)
+    normal = jnp.abs(moment1) >= 2.0**-14
+    ratio = jnp.where(normal, near / jnp.where(normal, moment1, 1.0), 1.0)
+    return near.astype(jnp.float16), (moment2 * ratio).astype(jnp.float16)
 
 
 def tree_sum(terms):
@@ -171,7 +178,7 @@
     blocks, rows, cols = own.shape
     owner = jnp.stack([lax.axis_index("dp"), lax.axis_index("mp") % 2]).astype(jnp.int32)
     full = (blocks, rows, cols)
-    tile = (8, cols)
+    tile = (1, cols)
 
     def send(x, axis, size, k):
         return lax.ppermute(x, axis, xor_pairs(size, k))
@@ -179,7 +186,7 @@
     def exchange(x, ks):
         return lax.ppermute(x, ("dp", "mp"), staged_pairs(replicas, shares, ks))
 
-    moments = jnp.stack([moment1, moment2]).astype(jnp.float16)[None]
+    moments = jnp.stack(near_moments(moment1, moment2))[None]
     offsets = [[0], [0]]
     carried = own
     for stage, ks in enumerate(STAGES):

time: 23.1 us -> 23.1 us (level)
    another operation x2 -> x1, other arithmetic: 0.79 us -> 0.81 us  [gathered(): moments = jnp.stack(near_moments(moment1, moment2))[None]]
where the time goes in v3:
time: 23.1 us; the launch traced here: 22.8 us
  starting transfers between devices  13.6 us (59%)
  waiting for transfers between devices  4.59 us (20%)
  Pallas kernels  2.21 us (10%)
  other arithmetic  1.06 us (5%)
  between operations  0.74 us (3%)
  local copies, waits for them, and re-layouts  0.63 us (3%)
    ppermute x6, starting transfers between devices, exchange(): return lax.ppermute(x, ('dp', 'mp'), staged_pairs(replicas, shares, ks))  11.6 us
    ppermute x6, waiting for transfers between devices, exchange(): return lax.ppermute(x, ('dp', 'mp'), staged_pairs(replicas, shares, ks))  3.67 us
    pallas_call x4, Pallas kernels, kernel_call(): pl.pallas_call(body, out_shape=out_shape, in_specs=[smem] * len(scalars)...  2.21 us
    ppermute x3, starting transfers between devices, send(): return lax.ppermute(x, axis, xor_pairs(size, k))  1.92 us
    ppermute x3, waiting for transfers between devices, send(): return lax.ppermute(x, axis, xor_pairs(size, k))  0.92 us
    another operation x1, other arithmetic, gathered(): moments = jnp.stack(near_moments(moment1, moment2))[None]  0.81 us
    unnamed x14, local copies, waits for them, and re-layouts  0.63 us
  transfers between devices with their start and end apart: 9, of which 6 were waited for; matrix products, arithmetic and copies ran while one was open for 5% of the time, Pallas kernels for 6%

profile of v3, /device:TPU:0, one launch (start us, length us, event | category | flops | bytes accessed | tf_op | source)
XLA Modules:
  0.0 22.8 jit_solution(15577185735089788358)
XLA Ops:
  0.6 4.1 %collective-permute-start = (bf16[8,32,128]{2,1,0:T(8,128)(2,1)}, bf16[8,32,128]{2,1,0:T(8,128)(2,1)S(1)}, u32[]{:S(2)}, u32[]{:S(2)}) collective-permute-start(bf16[8,32,128]{2,1,0:T(8,128)(2,1)} %bitcast.13), channel_id=1, source_target_pairs={{0,16},{1,5},{2,18},{3,7},{4,20},{5,1},{6,22},{7,3},{8,24},{9,13},... | collective-permute-start | bytes 196616 | tf_op jit(solution)/shard_map/ppermute | solution.py:187
  4.8 0.8 %fusion = (f16[1,2,32,128]{3,2,1,0:T(8,128)(2,1)S(1)}, f16[1,2,32,128]{3,2,1,0:T(8,128)(2,1)S(1)}) fusion(f32[2,32,128]{2,1,0:T(8,128)} %refs_12_.1, f32[2,32,128]{2,1,0:T(8,128)} %refs_13_.1), kind=kLoop, calls=%fused_computation.8 | loop fusion | flops 73728 | bytes 98304 | tf_op jit(solution)/shard_map/stack | solution.py:189
  5.6 0.1 collective-permute-start.6
  5.7 1.5 %collective-permute-done = bf16[8,32,128]{2,1,0:T(8,128)(2,1)S(1)} collective-permute-done((bf16[8,32,128]{2,1,0:T(8,128)(2,1)}, bf16[8,32,128]{2,1,0:T(8,128)(2,1)S(1)}, u32[]{:S(2)}, u32[]{:S(2)}) %collective-permute-start) | collective-permute-done | bytes 65568 | tf_op jit(solution)/shard_map/ppermute | solution.py:187
  7.2 2.3 %collective-permute-start.1 = (f32[8,32,128]{2,1,0:T(8,128)S(1)}, f32[8,32,128]{2,1,0:T(8,128)S(1)}, u32[]{:S(2)}, u32[]{:S(2)}) collective-permute-start(f32[8,32,128]{2,1,0:T(8,128)S(1)} %convert_add_fusion), channel_id=1, source_target_pairs={{0,8},{1,9},{2,10},{3,11},{4,12},{5,13},{6,14},{7,15},{8,0},{9,1},... | collective-permute-start | bytes 393224 | tf_op jit(solution)/shard_map/ppermute | solution.py:187
  9.5 1.1 %collective-permute-done.6 = f16[1,2,2,32,128]{4,3,2,1,0:T(8,128)(2,1)S(1)} collective-permute-done((f16[1,2,2,32,128]{4,3,2,1,0:T(8,128)(2,1)S(1)}, f16[1,2,2,32,128]{4,3,2,1,0:T(8,128)(2,1)S(1)}, u32[]{:S(2)}, u32[]{:S(2)}) %collective-permute-start.6) | collective-permute-done | bytes 32800 | tf_op jit(solution)/shard_map/ppermute | solution.py:187
  10.6 1.9 %collective-permute-start.7 = (f16[2,2,2,32,128]{4,3,2,1,0:T(8,128)(2,1)S(1)}, f16[2,2,2,32,128]{4,3,2,1,0:T(8,128)(2,1)S(1)}, u32[]{:S(2)}, u32[]{:S(2)}) collective-permute-start(f16[2,2,2,32,128]{4,3,2,1,0:T(8,128)(2,1)S(1)} %pad_maximum_fusion.1), channel_id=1, source_target_pairs={{0,8},{1,9},{2,10},{3,11},{4,12},{5,13},{6,14},{7,15},{8,0},{9,1},... | collective-permute-start | bytes 196616 | tf_op jit(solution)/shard_map/ppermute | solution.py:187
  12.5 1.7 %collective-permute-start.2 = (f32[8,32,128]{2,1,0:T(8,128)S(1)}, f32[8,32,128]{2,1,0:T(8,128)S(1)}, u32[]{:S(2)}, u32[]{:S(2)}) collective-permute-start(f32[8,32,128]{2,1,0:T(8,128)S(1)} %fusion.2.refs_0_), channel_id=1, source_target_pairs={{0,4},{1,17},{2,6},{3,19},{4,0},{5,21},{6,2},{7,23},{8,12},{9,25},... | collective-permute-start | bytes 393224 | tf_op jit(solution)/shard_map/ppermute | solution.py:187
  14.2 1.0 %collective-permute-done.7 = f16[2,2,2,32,128]{4,3,2,1,0:T(8,128)(2,1)S(1)} collective-permute-done((f16[2,2,2,32,128]{4,3,2,1,0:T(8,128)(2,1)S(1)}, f16[2,2,2,32,128]{4,3,2,1,0:T(8,128)(2,1)S(1)}, u32[]{:S(2)}, u32[]{:S(2)}) %collective-permute-start.7) | collective-permute-done | bytes 65568 | tf_op jit(solution)/shard_map/ppermute | solution.py:187
  15.3 1.6 %collective-permute-start.8 = (f16[4,2,2,32,128]{4,3,2,1,0:T(8,128)(2,1)S(1)}, f16[4,2,2,32,128]{4,3,2,1,0:T(8,128)(2,1)S(1)}, u32[]{:S(2)}, u32[]{:S(2)}) collective-permute-start(f16[4,2,2,32,128]{4,3,2,1,0:T(8,128)(2,1)S(1)} %pad_maximum_fusion), channel_id=1, source_target_pairs={{0,4},{1,17},{2,6},{3,19},{4,0},{5,21},{6,2},{7,23},{8,12},{9,25},... | collective-permute-start | bytes 393224 | tf_op jit(solution)/shard_map/ppermute | solution.py:187
  16.8 0.1 pad_add_fusion.owner_ref
  16.9 0.6 %copy-done.3 = s32[8]{0:T(128)S(1)} copy-done((s32[8]{0:T(128)S(1)}, s32[8]{0:T(128)}, u32[]{:S(2)}) %copy-start.3) | copy-done | bytes 56
  17.5 0.0 copy-done.5
  17.5 0.6 %shard_map.102 = (f32[8,32,128]{2,1,0:T(8,128)S(1)}, f32[1,128]{1,0:T(1,128)S(1)}, f32[8,32,128]{2,1,0:T(8,128)S(1)}) custom-call(s32[2]{0:T(128)S(1)} %pad_add_fusion.owner_ref, s32[8]{0:T(128)S(1)} %copy-done.3, s32[8]{0:T(128)S(1)} %copy-done.4, s32[8]{0:T(128)S(1)} %copy-done.5, bf16[8,32,128]{2,1,0:T(8,128)(2,1)S(1)} %copy-done.2), custom_call_target="tpu_custom_call" | custom-call | tf_op jit(solution)/shard_map/pallas_call | solution.py:59
  18.1 0.1 shard_map.103
  18.3 0.1 collective-permute-start.5
  18.4 1.6 %collective-permute-start.4 = (f32[1,128]{1,0:T(1,128)S(1)}, f32[1,128]{1,0:T(1,128)S(1)}, u32[]{:S(2)}, u32[]{:S(2)}) collective-permute-start(f32[1,128]{1,0:T(1,128)S(1)} %get-tuple-element.18.refs_0_), channel_id=1, source_target_pairs={{0,2},{1,3},{2,0},{3,1},{4,6},{5,7},{6,4},{7,5},{8,10},{9,11},{10,... | collective-permute-start | bytes 1544 | tf_op jit(solution)/shard_map/ppermute | solution.py:184
  19.9 0.3 %collective-permute-start.3 = (f32[1,128]{1,0:T(1,128)S(1)}, f32[1,128]{1,0:T(1,128)S(1)}, u32[]{:S(2)}, u32[]{:S(2)}) collective-permute-start(f32[1,128]{1,0:T(1,128)S(1)} %get-tuple-element.18.refs_0_), channel_id=1, source_target_pairs={{0,1},{1,0},{2,3},{3,2},{4,5},{5,4},{6,7},{7,6},{8,9},{9,8},{10,11... | collective-permute-start | bytes 1544 | tf_op jit(solution)/shard_map/ppermute | solution.py:184
  20.2 0.1 collective-permute-done.8
  20.3 0.1 maximum_convert_fusion.moments_ref
  20.4 0.7 %shard_map.104 = (f32[8,32,128]{2,1,0:T(8,128)S(1)}, f32[8,32,128]{2,1,0:T(8,128)S(1)}, f32[2,32,128]{2,1,0:T(8,128)S(1)}, f32[2,32,128]{2,1,0:T(8,128)S(1)}) custom-call(s32[2]{0:T(128)S(1)} %pad_add_fusion.owner_ref, s32[8]{0:T(128)S(1)} %copy-done.3, f32[8,32,128]{2,1,0:T(8,128)S(1)} %get-tuple-element.19.total_ref.refs_4_, ...), custom_call_target="tpu_custom_call" | custom-call | tf_op jit(solution)/shard_map/pallas_call | solution.py:59
  21.1 0.3 %collective-permute-done.5.refs_3_ = f32[1,128]{1,0:T(1,128)S(1)} collective-permute-done((f32[1,128]{1,0:T(1,128)S(1)}, f32[1,128]{1,0:T(1,128)S(1)}, u32[]{:S(2)}, u32[]{:S(2)}) %collective-permute-start.5) | collective-permute-done | bytes 544 | tf_op jit(solution)/shard_map/ppermute | solution.py:184
  21.3 0.7 %collective-permute-done.4.refs_2_ = f32[1,128]{1,0:T(1,128)S(1)} collective-permute-done((f32[1,128]{1,0:T(1,128)S(1)}, f32[1,128]{1,0:T(1,128)S(1)}, u32[]{:S(2)}, u32[]{:S(2)}) %collective-permute-start.4) | collective-permute-done | bytes 544 | tf_op jit(solution)/shard_map/ppermute | solution.py:184
  22.0 0.8 %shard_map.105 = (f32[2,32,128]{2,1,0:T(8,128)}, f32[2,32,128]{2,1,0:T(8,128)}, bf16[8,32,128]{2,1,0:T(8,128)(2,1)}, f32[1]{0:T(128)}) custom-call(f32[1,128]{1,0:T(1,128)S(1)} %get-tuple-element.18.refs_0_, f32[1,128]{1,0:T(1,128)S(1)} %collective-permute-done.3.refs_1_, f32[1,128]{1,0:T(1,128)S(1)} %collective-permute-done.4.refs_2_, ...), custom_call_target="tpu_custom_call" | custom-call | tf_op jit(solution)/shard_map/pallas_call | solution.py:59
  (20 shorter events, 0.2 us)
Async XLA Ops:
  0.6 6.6 %copy-start.6 = (bf16[1,8,32,128]{3,2,1,0:T(8,128)(2,1)S(1)}, bf16[1,8,32,128]{3,2,1,0:T(8,128)(2,1)}, u32[]{:S(2)}) copy-start(bf16[1,8,32,128]{3,2,1,0:T(8,128)(2,1)} %param.7) | copy-start | bytes 196612
  0.6 6.6 %collective-permute-start = (bf16[8,32,128]{2,1,0:T(8,128)(2,1)}, bf16[8,32,128]{2,1,0:T(8,128)(2,1)S(1)}, u32[]{:S(2)}, u32[]{:S(2)}) collective-permute-start(bf16[8,32,128]{2,1,0:T(8,128)(2,1)} %bitcast.13), channel_id=1, source_target_pairs={{0,16},{1,5},{2,18},{3,7},{4,20},{5,1},{6,22},{7,3},{8,24},{9,13},... | collective-permute-start | bytes 196616 | tf_op jit(solution)/shard_map/ppermute | solution.py:187
  5.6 5.0 %collective-permute-start.6 = (f16[1,2,2,32,128]{4,3,2,1,0:T(8,128)(2,1)S(1)}, f16[1,2,2,32,128]{4,3,2,1,0:T(8,128)(2,1)S(1)}, u32[]{:S(2)}, u32[]{:S(2)}) collective-permute-start(f16[1,2,2,32,128]{4,3,2,1,0:T(8,128)(2,1)S(1)} %maximum_bitcast_fusion), channel_id=1, source_target_pairs={{0,16},{1,5},{2,18},{3,7},{4,20},{5,1},{6,22},{7,3},{8,24},{9,13},... | collective-permute-start | bytes 98312 | tf_op jit(solution)/shard_map/ppermute | solution.py:187
  7.2 5.2 %collective-permute-start.1 = (f32[8,32,128]{2,1,0:T(8,128)S(1)}, f32[8,32,128]{2,1,0:T(8,128)S(1)}, u32[]{:S(2)}, u32[]{:S(2)}) collective-permute-start(f32[8,32,128]{2,1,0:T(8,128)S(1)} %convert_add_fusion), channel_id=1, source_target_pairs={{0,8},{1,9},{2,10},{3,11},{4,12},{5,13},{6,14},{7,15},{8,0},{9,1},... | collective-permute-start | bytes 393224 | tf_op jit(solution)/shard_map/ppermute | solution.py:187
  10.6 4.6 %collective-permute-start.7 = (f16[2,2,2,32,128]{4,3,2,1,0:T(8,128)(2,1)S(1)}, f16[2,2,2,32,128]{4,3,2,1,0:T(8,128)(2,1)S(1)}, u32[]{:S(2)}, u32[]{:S(2)}) collective-permute-start(f16[2,2,2,32,128]{4,3,2,1,0:T(8,128)(2,1)S(1)} %pad_maximum_fusion.1), channel_id=1, source_target_pairs={{0,8},{1,9},{2,10},{3,11},{4,12},{5,13},{6,14},{7,15},{8,0},{9,1},... | collective-permute-start | bytes 196616 | tf_op jit(solution)/shard_map/ppermute | solution.py:187
  12.5 5.6 %collective-permute-start.2 = (f32[8,32,128]{2,1,0:T(8,128)S(1)}, f32[8,32,128]{2,1,0:T(8,128)S(1)}, u32[]{:S(2)}, u32[]{:S(2)}) collective-permute-start(f32[8,32,128]{2,1,0:T(8,128)S(1)} %fusion.2.refs_0_), channel_id=1, source_target_pairs={{0,4},{1,17},{2,6},{3,19},{4,0},{5,21},{6,2},{7,23},{8,12},{9,25},... | collective-permute-start | bytes 393224 | tf_op jit(solution)/shard_map/ppermute | solution.py:187
  15.2 1.7 %copy-start.2 = (bf16[8,32,128]{2,1,0:T(8,128)(2,1)S(1)}, bf16[8,32,128]{2,1,0:T(8,128)(2,1)}, u32[]{:S(2)}) copy-start(bf16[8,32,128]{2,1,0:T(8,128)(2,1)} %weight_ref.1) | copy-start | bytes 196612
  15.3 5.0 %collective-permute-start.8 = (f16[4,2,2,32,128]{4,3,2,1,0:T(8,128)(2,1)S(1)}, f16[4,2,2,32,128]{4,3,2,1,0:T(8,128)(2,1)S(1)}, u32[]{:S(2)}, u32[]{:S(2)}) collective-permute-start(f16[4,2,2,32,128]{4,3,2,1,0:T(8,128)(2,1)S(1)} %pad_maximum_fusion), channel_id=1, source_target_pairs={{0,4},{1,17},{2,6},{3,19},{4,0},{5,21},{6,2},{7,23},{8,12},{9,25},... | collective-permute-start | bytes 393224 | tf_op jit(solution)/shard_map/ppermute | solution.py:187
  16.8 0.7 %copy-start.3 = (s32[8]{0:T(128)S(1)}, s32[8]{0:T(128)}, u32[]{:S(2)}) copy-start(s32[8]{0:T(128)} %slot_ref.3) | copy-start | bytes 100
  16.8 0.7 %copy-start.4 = (s32[8]{0:T(128)S(1)}, s32[8]{0:T(128)}, u32[]{:S(2)}) copy-start(s32[8]{0:T(128)} %trainable_ref.1) | copy-start | bytes 100
  16.8 0.7 %copy-start.5 = (s32[8]{0:T(128)S(1)}, s32[8]{0:T(128)}, u32[]{:S(2)}) copy-start(s32[8]{0:T(128)} %width_ref.1) | copy-start | bytes 100
  18.3 3.1 %collective-permute-start.5 = (f32[1,128]{1,0:T(1,128)S(1)}, f32[1,128]{1,0:T(1,128)S(1)}, u32[]{:S(2)}, u32[]{:S(2)}) collective-permute-start(f32[1,128]{1,0:T(1,128)S(1)} %get-tuple-element.18.refs_0_), channel_id=1, source_target_pairs={{0,3},{1,2},{2,1},{3,0},{4,7},{5,6},{6,5},{7,4},{8,11},{9,10},{10,... | collective-permute-start | bytes 1544 | tf_op jit(solution)/shard_map/ppermute | solution.py:184
  18.4 3.6 %collective-permute-start.4 = (f32[1,128]{1,0:T(1,128)S(1)}, f32[1,128]{1,0:T(1,128)S(1)}, u32[]{:S(2)}, u32[]{:S(2)}) collective-permute-start(f32[1,128]{1,0:T(1,128)S(1)} %get-tuple-element.18.refs_0_), channel_id=1, source_target_pairs={{0,2},{1,3},{2,0},{3,1},{4,6},{5,7},{6,4},{7,5},{8,10},{9,11},{10,... | collective-permute-start | bytes 1544 | tf_op jit(solution)/shard_map/ppermute | solution.py:184
  19.9 2.1 %collective-permute-start.3 = (f32[1,128]{1,0:T(1,128)S(1)}, f32[1,128]{1,0:T(1,128)S(1)}, u32[]{:S(2)}, u32[]{:S(2)}) collective-permute-start(f32[1,128]{1,0:T(1,128)S(1)} %get-tuple-element.18.refs_0_), channel_id=1, source_target_pairs={{0,1},{1,0},{2,3},{3,2},{4,5},{5,4},{6,7},{7,6},{8,9},{9,8},{10,11... | collective-permute-start | bytes 1544 | tf_op jit(solution)/shard_map/ppermute | solution.py:184
  20.4 1.6 %copy-start = (f32[2,32,128]{2,1,0:T(8,128)S(1)}, f32[2,32,128]{2,1,0:T(8,128)}, u32[]{:S(2)}) copy-start(f32[2,32,128]{2,1,0:T(8,128)} %refs_12_.1) | copy-start | bytes 98308
  20.4 1.6 %copy-start.1 = (f32[2,32,128]{2,1,0:T(8,128)S(1)}, f32[2,32,128]{2,1,0:T(8,128)}, u32[]{:S(2)}) copy-start(f32[2,32,128]{2,1,0:T(8,128)} %refs_13_.1) | copy-start | bytes 98308

commit v4 on v3

--- a/solution.py
+++ b/solution.py
@@ -159,7 +159,10 @@
         second_new = block_second_ref[b] + 0.05 * clipped * clipped
         spread = jnp.sqrt(second_new * (1.0 / (1.0 - 0.95**STEP))) + 1e-08
         change = first_new * (RATE / (1.0 - 0.9**STEP)) / spread
-        weight_out[b] = (wide_ref[b] - change * live_ref[b]).astype(weight_out.dtype)
+        kept = wide_ref[b]
+        weight_out[b] = jnp.where(live_ref[b] > 0, kept - change, kept).astype(
+            weight_out.dtype
+        )
     rms_out[0] = jnp.max(grad_rms)
 
 

time: 23.1 us -> 23.1 us (level)
  no operation moved by 1% of the time
where the time goes in v4:
time: 23.1 us; the launch traced here: 22.8 us
  starting transfers between devices  13.6 us (59%)
  waiting for transfers between devices  4.59 us (20%)
  Pallas kernels  2.21 us (10%)
  other arithmetic  1.06 us (5%)
  between operations  0.74 us (3%)
  local copies, waits for them, and re-layouts  0.63 us (3%)
    ppermute x6, starting transfers between devices, exchange(): return lax.ppermute(x, ('dp', 'mp'), staged_pairs(replicas, shares, ks))  11.6 us
    ppermute x6, waiting for transfers between devices, exchange(): return lax.ppermute(x, ('dp', 'mp'), staged_pairs(replicas, shares, ks))  3.67 us
    pallas_call x4, Pallas kernels, kernel_call(): pl.pallas_call(body, out_shape=out_shape, in_specs=[smem] * len(scalars)...  2.21 us
    ppermute x3, starting transfers between devices, send(): return lax.ppermute(x, axis, xor_pairs(size, k))  1.92 us
    ppermute x3, waiting for transfers between devices, send(): return lax.ppermute(x, axis, xor_pairs(size, k))  0.92 us
    another operation x1, other arithmetic, gathered(): moments = jnp.stack(near_moments(moment1, moment2))[None]  0.81 us
    unnamed x14, local copies, waits for them, and re-layouts  0.63 us
  transfers between devices with their start and end apart: 9, of which 6 were waited for; matrix products, arithmetic and copies ran while one was open for 5% of the time, Pallas kernels for 6%

profile of v4, /device:TPU:0, one launch (start us, length us, event | category | flops | bytes accessed | tf_op | source)
XLA Modules:
  0.0 22.8 jit_solution(7744084064154898751)
XLA Ops:
  0.6 4.1 %collective-permute-start = (bf16[8,32,128]{2,1,0:T(8,128)(2,1)}, bf16[8,32,128]{2,1,0:T(8,128)(2,1)S(1)}, u32[]{:S(2)}, u32[]{:S(2)}) collective-permute-start(bf16[8,32,128]{2,1,0:T(8,128)(2,1)} %bitcast.13), channel_id=1, source_target_pairs={{0,16},{1,5},{2,18},{3,7},{4,20},{5,1},{6,22},{7,3},{8,24},{9,13},... | collective-permute-start | bytes 196616 | tf_op jit(solution)/shard_map/ppermute | solution.py:190
  4.8 0.8 %fusion = (f16[1,2,32,128]{3,2,1,0:T(8,128)(2,1)S(1)}, f16[1,2,32,128]{3,2,1,0:T(8,128)(2,1)S(1)}) fusion(f32[2,32,128]{2,1,0:T(8,128)} %refs_12_.1, f32[2,32,128]{2,1,0:T(8,128)} %refs_13_.1), kind=kLoop, calls=%fused_computation.8 | loop fusion | flops 73728 | bytes 98304 | tf_op jit(solution)/shard_map/stack | solution.py:192
  5.6 0.1 collective-permute-start.6
  5.7 1.5 %collective-permute-done = bf16[8,32,128]{2,1,0:T(8,128)(2,1)S(1)} collective-permute-done((bf16[8,32,128]{2,1,0:T(8,128)(2,1)}, bf16[8,32,128]{2,1,0:T(8,128)(2,1)S(1)}, u32[]{:S(2)}, u32[]{:S(2)}) %collective-permute-start) | collective-permute-done | bytes 65568 | tf_op jit(solution)/shard_map/ppermute | solution.py:190
  7.2 2.3 %collective-permute-start.1 = (f32[8,32,128]{2,1,0:T(8,128)S(1)}, f32[8,32,128]{2,1,0:T(8,128)S(1)}, u32[]{:S(2)}, u32[]{:S(2)}) collective-permute-start(f32[8,32,128]{2,1,0:T(8,128)S(1)} %convert_add_fusion), channel_id=1, source_target_pairs={{0,8},{1,9},{2,10},{3,11},{4,12},{5,13},{6,14},{7,15},{8,0},{9,1},... | collective-permute-start | bytes 393224 | tf_op jit(solution)/shard_map/ppermute | solution.py:190
  9.5 1.1 %collective-permute-done.6 = f16[1,2,2,32,128]{4,3,2,1,0:T(8,128)(2,1)S(1)} collective-permute-done((f16[1,2,2,32,128]{4,3,2,1,0:T(8,128)(2,1)S(1)}, f16[1,2,2,32,128]{4,3,2,1,0:T(8,128)(2,1)S(1)}, u32[]{:S(2)}, u32[]{:S(2)}) %collective-permute-start.6) | collective-permute-done | bytes 32800 | tf_op jit(solution)/shard_map/ppermute | solution.py:190
  10.6 1.9 %collective-permute-start.7 = (f16[2,2,2,32,128]{4,3,2,1,0:T(8,128)(2,1)S(1)}, f16[2,2,2,32,128]{4,3,2,1,0:T(8,128)(2,1)S(1)}, u32[]{:S(2)}, u32[]{:S(2)}) collective-permute-start(f16[2,2,2,32,128]{4,3,2,1,0:T(8,128)(2,1)S(1)} %pad_maximum_fusion.1), channel_id=1, source_target_pairs={{0,8},{1,9},{2,10},{3,11},{4,12},{5,13},{6,14},{7,15},{8,0},{9,1},... | collective-permute-start | bytes 196616 | tf_op jit(solution)/shard_map/ppermute | solution.py:190
  12.5 1.7 %collective-permute-start.2 = (f32[8,32,128]{2,1,0:T(8,128)S(1)}, f32[8,32,128]{2,1,0:T(8,128)S(1)}, u32[]{:S(2)}, u32[]{:S(2)}) collective-permute-start(f32[8,32,128]{2,1,0:T(8,128)S(1)} %fusion.2.refs_0_), channel_id=1, source_target_pairs={{0,4},{1,17},{2,6},{3,19},{4,0},{5,21},{6,2},{7,23},{8,12},{9,25},... | collective-permute-start | bytes 393224 | tf_op jit(solution)/shard_map/ppermute | solution.py:190
  14.2 1.0 %collective-permute-done.7 = f16[2,2,2,32,128]{4,3,2,1,0:T(8,128)(2,1)S(1)} collective-permute-done((f16[2,2,2,32,128]{4,3,2,1,0:T(8,128)(2,1)S(1)}, f16[2,2,2,32,128]{4,3,2,1,0:T(8,128)(2,1)S(1)}, u32[]{:S(2)}, u32[]{:S(2)}) %collective-permute-start.7) | collective-permute-done | bytes 65568 | tf_op jit(solution)/shard_map/ppermute | solution.py:190
  15.3 1.6 %collective-permute-start.8 = (f16[4,2,2,32,128]{4,3,2,1,0:T(8,128)(2,1)S(1)}, f16[4,2,2,32,128]{4,3,2,1,0:T(8,128)(2,1)S(1)}, u32[]{:S(2)}, u32[]{:S(2)}) collective-permute-start(f16[4,2,2,32,128]{4,3,2,1,0:T(8,128)(2,1)S(1)} %pad_maximum_fusion), channel_id=1, source_target_pairs={{0,4},{1,17},{2,6},{3,19},{4,0},{5,21},{6,2},{7,23},{8,12},{9,25},... | collective-permute-start | bytes 393224 | tf_op jit(solution)/shard_map/ppermute | solution.py:190
  16.8 0.1 pad_add_fusion.owner_ref
  16.9 0.6 %copy-done.3 = s32[8]{0:T(128)S(1)} copy-done((s32[8]{0:T(128)S(1)}, s32[8]{0:T(128)}, u32[]{:S(2)}) %copy-start.3) | copy-done | bytes 56
  17.5 0.0 copy-done.5
  17.5 0.6 %shard_map.102 = (f32[8,32,128]{2,1,0:T(8,128)S(1)}, f32[1,128]{1,0:T(1,128)S(1)}, f32[8,32,128]{2,1,0:T(8,128)S(1)}) custom-call(s32[2]{0:T(128)S(1)} %pad_add_fusion.owner_ref, s32[8]{0:T(128)S(1)} %copy-done.3, s32[8]{0:T(128)S(1)} %copy-done.4, s32[8]{0:T(128)S(1)} %copy-done.5, bf16[8,32,128]{2,1,0:T(8,128)(2,1)S(1)} %copy-done.2), custom_call_target="tpu_custom_call" | custom-call | tf_op jit(solution)/shard_map/pallas_call | solution.py:59
  18.1 0.1 shard_map.103
  18.3 0.1 collective-permute-start.5
  18.4 1.6 %collective-permute-start.4 = (f32[1,128]{1,0:T(1,128)S(1)}, f32[1,128]{1,0:T(1,128)S(1)}, u32[]{:S(2)}, u32[]{:S(2)}) collective-permute-start(f32[1,128]{1,0:T(1,128)S(1)} %get-tuple-element.18.refs_0_), channel_id=1, source_target_pairs={{0,2},{1,3},{2,0},{3,1},{4,6},{5,7},{6,4},{7,5},{8,10},{9,11},{10,... | collective-permute-start | bytes 1544 | tf_op jit(solution)/shard_map/ppermute | solution.py:187
  19.9 0.3 %collective-permute-start.3 = (f32[1,128]{1,0:T(1,128)S(1)}, f32[1,128]{1,0:T(1,128)S(1)}, u32[]{:S(2)}, u32[]{:S(2)}) collective-permute-start(f32[1,128]{1,0:T(1,128)S(1)} %get-tuple-element.18.refs_0_), channel_id=1, source_target_pairs={{0,1},{1,0},{2,3},{3,2},{4,5},{5,4},{6,7},{7,6},{8,9},{9,8},{10,11... | collective-permute-start | bytes 1544 | tf_op jit(solution)/shard_map/ppermute | solution.py:187
  20.2 0.1 collective-permute-done.8
  20.3 0.1 maximum_convert_fusion.moments_ref
  20.4 0.7 %shard_map.104 = (f32[8,32,128]{2,1,0:T(8,128)S(1)}, f32[8,32,128]{2,1,0:T(8,128)S(1)}, f32[2,32,128]{2,1,0:T(8,128)S(1)}, f32[2,32,128]{2,1,0:T(8,128)S(1)}) custom-call(s32[2]{0:T(128)S(1)} %pad_add_fusion.owner_ref, s32[8]{0:T(128)S(1)} %copy-done.3, f32[8,32,128]{2,1,0:T(8,128)S(1)} %get-tuple-element.19.total_ref.refs_4_, ...), custom_call_target="tpu_custom_call" | custom-call | tf_op jit(solution)/shard_map/pallas_call | solution.py:59
  21.1 0.3 %collective-permute-done.5.refs_3_ = f32[1,128]{1,0:T(1,128)S(1)} collective-permute-done((f32[1,128]{1,0:T(1,128)S(1)}, f32[1,128]{1,0:T(1,128)S(1)}, u32[]{:S(2)}, u32[]{:S(2)}) %collective-permute-start.5) | collective-permute-done | bytes 544 | tf_op jit(solution)/shard_map/ppermute | solution.py:187
  21.3 0.7 %collective-permute-done.4.refs_2_ = f32[1,128]{1,0:T(1,128)S(1)} collective-permute-done((f32[1,128]{1,0:T(1,128)S(1)}, f32[1,128]{1,0:T(1,128)S(1)}, u32[]{:S(2)}, u32[]{:S(2)}) %collective-permute-start.4) | collective-permute-done | bytes 544 | tf_op jit(solution)/shard_map/ppermute | solution.py:187
  22.0 0.8 %shard_map.105 = (f32[2,32,128]{2,1,0:T(8,128)}, f32[2,32,128]{2,1,0:T(8,128)}, bf16[8,32,128]{2,1,0:T(8,128)(2,1)}, f32[1]{0:T(128)}) custom-call(f32[1,128]{1,0:T(1,128)S(1)} %get-tuple-element.18.refs_0_, f32[1,128]{1,0:T(1,128)S(1)} %collective-permute-done.3.refs_1_, f32[1,128]{1,0:T(1,128)S(1)} %collective-permute-done.4.refs_2_, ...), custom_call_target="tpu_custom_call" | custom-call | tf_op jit(solution)/shard_map/pallas_call | solution.py:59
  (20 shorter events, 0.2 us)
Async XLA Ops:
  0.6 6.6 %copy-start.6 = (bf16[1,8,32,128]{3,2,1,0:T(8,128)(2,1)S(1)}, bf16[1,8,32,128]{3,2,1,0:T(8,128)(2,1)}, u32[]{:S(2)}) copy-start(bf16[1,8,32,128]{3,2,1,0:T(8,128)(2,1)} %param.7) | copy-start | bytes 196612
  0.6 6.6 %collective-permute-start = (bf16[8,32,128]{2,1,0:T(8,128)(2,1)}, bf16[8,32,128]{2,1,0:T(8,128)(2,1)S(1)}, u32[]{:S(2)}, u32[]{:S(2)}) collective-permute-start(bf16[8,32,128]{2,1,0:T(8,128)(2,1)} %bitcast.13), channel_id=1, source_target_pairs={{0,16},{1,5},{2,18},{3,7},{4,20},{5,1},{6,22},{7,3},{8,24},{9,13},... | collective-permute-start | bytes 196616 | tf_op jit(solution)/shard_map/ppermute | solution.py:190
  5.6 5.0 %collective-permute-start.6 = (f16[1,2,2,32,128]{4,3,2,1,0:T(8,128)(2,1)S(1)}, f16[1,2,2,32,128]{4,3,2,1,0:T(8,128)(2,1)S(1)}, u32[]{:S(2)}, u32[]{:S(2)}) collective-permute-start(f16[1,2,2,32,128]{4,3,2,1,0:T(8,128)(2,1)S(1)} %maximum_bitcast_fusion), channel_id=1, source_target_pairs={{0,16},{1,5},{2,18},{3,7},{4,20},{5,1},{6,22},{7,3},{8,24},{9,13},... | collective-permute-start | bytes 98312 | tf_op jit(solution)/shard_map/ppermute | solution.py:190
  7.2 5.2 %collective-permute-start.1 = (f32[8,32,128]{2,1,0:T(8,128)S(1)}, f32[8,32,128]{2,1,0:T(8,128)S(1)}, u32[]{:S(2)}, u32[]{:S(2)}) collective-permute-start(f32[8,32,128]{2,1,0:T(8,128)S(1)} %convert_add_fusion), channel_id=1, source_target_pairs={{0,8},{1,9},{2,10},{3,11},{4,12},{5,13},{6,14},{7,15},{8,0},{9,1},... | collective-permute-start | bytes 393224 | tf_op jit(solution)/shard_map/ppermute | solution.py:190
  10.6 4.6 %collective-permute-start.7 = (f16[2,2,2,32,128]{4,3,2,1,0:T(8,128)(2,1)S(1)}, f16[2,2,2,32,128]{4,3,2,1,0:T(8,128)(2,1)S(1)}, u32[]{:S(2)}, u32[]{:S(2)}) collective-permute-start(f16[2,2,2,32,128]{4,3,2,1,0:T(8,128)(2,1)S(1)} %pad_maximum_fusion.1), channel_id=1, source_target_pairs={{0,8},{1,9},{2,10},{3,11},{4,12},{5,13},{6,14},{7,15},{8,0},{9,1},... | collective-permute-start | bytes 196616 | tf_op jit(solution)/shard_map/ppermute | solution.py:190
  12.5 5.6 %collective-permute-start.2 = (f32[8,32,128]{2,1,0:T(8,128)S(1)}, f32[8,32,128]{2,1,0:T(8,128)S(1)}, u32[]{:S(2)}, u32[]{:S(2)}) collective-permute-start(f32[8,32,128]{2,1,0:T(8,128)S(1)} %fusion.2.refs_0_), channel_id=1, source_target_pairs={{0,4},{1,17},{2,6},{3,19},{4,0},{5,21},{6,2},{7,23},{8,12},{9,25},... | collective-permute-start | bytes 393224 | tf_op jit(solution)/shard_map/ppermute | solution.py:190
  15.2 1.7 %copy-start.2 = (bf16[8,32,128]{2,1,0:T(8,128)(2,1)S(1)}, bf16[8,32,128]{2,1,0:T(8,128)(2,1)}, u32[]{:S(2)}) copy-start(bf16[8,32,128]{2,1,0:T(8,128)(2,1)} %weight_ref.1) | copy-start | bytes 196612
  15.3 5.0 %collective-permute-start.8 = (f16[4,2,2,32,128]{4,3,2,1,0:T(8,128)(2,1)S(1)}, f16[4,2,2,32,128]{4,3,2,1,0:T(8,128)(2,1)S(1)}, u32[]{:S(2)}, u32[]{:S(2)}) collective-permute-start(f16[4,2,2,32,128]{4,3,2,1,0:T(8,128)(2,1)S(1)} %pad_maximum_fusion), channel_id=1, source_target_pairs={{0,4},{1,17},{2,6},{3,19},{4,0},{5,21},{6,2},{7,23},{8,12},{9,25},... | collective-permute-start | bytes 393224 | tf_op jit(solution)/shard_map/ppermute | solution.py:190
  16.8 0.7 %copy-start.3 = (s32[8]{0:T(128)S(1)}, s32[8]{0:T(128)}, u32[]{:S(2)}) copy-start(s32[8]{0:T(128)} %slot_ref.3) | copy-start | bytes 100
  16.8 0.7 %copy-start.4 = (s32[8]{0:T(128)S(1)}, s32[8]{0:T(128)}, u32[]{:S(2)}) copy-start(s32[8]{0:T(128)} %trainable_ref.1) | copy-start | bytes 100
  16.8 0.7 %copy-start.5 = (s32[8]{0:T(128)S(1)}, s32[8]{0:T(128)}, u32[]{:S(2)}) copy-start(s32[8]{0:T(128)} %width_ref.1) | copy-start | bytes 100
  18.3 3.1 %collective-permute-start.5 = (f32[1,128]{1,0:T(1,128)S(1)}, f32[1,128]{1,0:T(1,128)S(1)}, u32[]{:S(2)}, u32[]{:S(2)}) collective-permute-start(f32[1,128]{1,0:T(1,128)S(1)} %get-tuple-element.18.refs_0_), channel_id=1, source_target_pairs={{0,3},{1,2},{2,1},{3,0},{4,7},{5,6},{6,5},{7,4},{8,11},{9,10},{10,... | collective-permute-start | bytes 1544 | tf_op jit(solution)/shard_map/ppermute | solution.py:187
  18.4 3.6 %collective-permute-start.4 = (f32[1,128]{1,0:T(1,128)S(1)}, f32[1,128]{1,0:T(1,128)S(1)}, u32[]{:S(2)}, u32[]{:S(2)}) collective-permute-start(f32[1,128]{1,0:T(1,128)S(1)} %get-tuple-element.18.refs_0_), channel_id=1, source_target_pairs={{0,2},{1,3},{2,0},{3,1},{4,6},{5,7},{6,4},{7,5},{8,10},{9,11},{10,... | collective-permute-start | bytes 1544 | tf_op jit(solution)/shard_map/ppermute | solution.py:187
  19.9 2.1 %collective-permute-start.3 = (f32[1,128]{1,0:T(1,128)S(1)}, f32[1,128]{1,0:T(1,128)S(1)}, u32[]{:S(2)}, u32[]{:S(2)}) collective-permute-start(f32[1,128]{1,0:T(1,128)S(1)} %get-tuple-element.18.refs_0_), channel_id=1, source_target_pairs={{0,1},{1,0},{2,3},{3,2},{4,5},{5,4},{6,7},{7,6},{8,9},{9,8},{10,11... | collective-permute-start | bytes 1544 | tf_op jit(solution)/shard_map/ppermute | solution.py:187
  20.4 1.6 %copy-start = (f32[2,32,128]{2,1,0:T(8,128)S(1)}, f32[2,32,128]{2,1,0:T(8,128)}, u32[]{:S(2)}) copy-start(f32[2,32,128]{2,1,0:T(8,128)} %refs_12_.1) | copy-start | bytes 98308
  20.4 1.6 %copy-start.1 = (f32[2,32,128]{2,1,0:T(8,128)S(1)}, f32[2,32,128]{2,1,0:T(8,128)}, u32[]{:S(2)}) copy-start(f32[2,32,128]{2,1,0:T(8,128)} %refs_13_.1) | copy-start | bytes 98308
